TPU v7x, 512 devices: a whole 4x8x8 slice. The times are simulated.
512 devices in a mesh: dp: 64 (over y, z), mp: 8 (over x, core).
Axes of the slice: x: 4, y: 8, z: 8, core: 2. Of those that a mesh axis runs over, the one named last changes fastest.
Arguments:
- hidden: bfloat16 [8192, 4096], P('dp', 'mp'), may hold values from -6 to 6
- attended: bfloat16 [8192, 4096], P('dp', 'mp'), may hold values from -6 to 6
- query_cotangent: bfloat16 [8192, 4096], P('dp', 'mp'), may hold values from -1.5 to 1.5
- output_cotangent: bfloat16 [8192, 4096], P('dp', 'mp'), may hold values from -1.5 to 1.5
- query_projection_weight: bfloat16 [4096, 4096], P('dp', 'mp'), may hold values from -0.09375 to 0.09375
- output_projection_weight: bfloat16 [4096, 4096], P('dp', 'mp'), may hold values from -0.09375 to 0.09375
- narrower: bfloat16 [1024, 16, 4096], P('dp', None, 'mp'), may hold values from -0.09375 to 0.09375
- widener: bfloat16 [1024, 16, 4096], P('dp', None, 'mp'), may hold values from -0.375 to 0.375
- reducer: bfloat16 [1024, 16, 4096], P('dp', None, 'mp'), may hold values from -0.09375 to 0.09375
- enlarger: bfloat16 [1024, 16, 4096], P('dp', None, 'mp'), may hold values from -0.375 to 0.375
- block_adapter: int32 [2048], P('dp'), may hold values from 0 to 1023, as said below
- block_fill: int32 [2048], P('dp'), may hold values from 1 to 4
Outputs:
- queries: bfloat16 [8192, 4096], P('dp', 'mp')
- projected: bfloat16 [8192, 4096], P('dp', 'mp')
- hidden_state_gradient: bfloat16 [8192, 4096], P('dp', 'mp')
- attention_output_gradient: bfloat16 [8192, 4096], P('dp', 'mp')
- narrower_gradient: float32 [1024, 16, 4096], P('dp', None, 'mp')
- widener_gradient: float32 [1024, 16, 4096], P('dp', None, 'mp')
- reducer_gradient: float32 [1024, 16, 4096], P('dp', None, 'mp')
- enlarger_gradient: float32 [1024, 16, 4096], P('dp', None, 'mp')
Inputs may be any that keep to these rules, and one draw needn't show every extreme that they name: `block_adapter`: the owner of adapter e is e // 16. Among the 32 blocks of one group (one index of dp), at most 1 have adapters of one owner, and some owner has exactly 1 block in every group.
All inputs are finite; a program needn't handle non-finite values.
Results may differ from a plain program's by a relative error of at most 0.015.
Values may be sent and summed in bfloat16 or wider, within the bound.
No kernel may reach another device: no remote copies, remote signals or barrier semaphores. Data moves between devices by JAX's collectives and lax.ppermute only.
A program may use at most 64 MiB of HBM per device.

v0:
```python
import math

import jax
import jax.numpy as jnp
from jax import lax
from jax.sharding import PartitionSpec as P

adapter_scale = 2.0


def side_by_side(arrays, axis, dim, along):
    both = jnp.concatenate(arrays, axis=along)
    result, at, done = (lax.all_gather(both, axis, axis=dim, tiled=True), 0, [])
    for a in arrays:
        done.append(lax.slice_in_dim(result, at, at + a.shape[along], axis=along))
        at += a.shape[along]
    return tuple(done)


def in_one_piece(arrays, axis, dim, along):
    both = jnp.concatenate(arrays, axis=along)
    result, at, done = (lax.psum_scatter(both, axis, scatter_dimension=dim, tiled=True), 0, [])
    for a in arrays:
        done.append(lax.slice_in_dim(result, at, at + a.shape[along], axis=along))
        at += a.shape[along]
    return tuple(done)


def sent_together(arrays, axis, split_dim, concat_dim, along):
    widths = [math.prod(a.shape[along:]) for a in arrays]
    both = jnp.concatenate(
        [a.reshape(*a.shape[:along], w) for a, w in zip(arrays, widths)], axis=along
    )
    result = lax.all_to_all(both, axis, split_axis=split_dim, concat_axis=concat_dim, tiled=True)
    blocks = jnp.split(result, [sum(widths[:k]) for k in range(1, len(widths))], axis=along)
    return tuple(
        (b.reshape(*result.shape[:along], *a.shape[along:]) for a, b in zip(arrays, blocks))
    )


def copy_for_each(array, axis):
    copies = jnp.broadcast_to(array, (lax.axis_size(axis), *array.shape))
    return lax.all_to_all(copies, axis, split_axis=0, concat_axis=0, tiled=True)


def of_everyone(array, axis):
    everything = copy_for_each(array, axis)
    return jnp.sum(everything.astype(jnp.float32), axis=0)


def sent_together_2(arrays, axis, split_dim, concat_dim, along):
    ends, at = ([], 0)
    for a in arrays[:-1]:
        at += a.shape[along]
        ends.append(at)
    both = jnp.concatenate(arrays, axis=along)
    return tuple(
        jnp.split(
            lax.all_to_all(both, axis, split_axis=split_dim, concat_axis=concat_dim, tiled=True),
            ends,
            axis=along,
        )
    )


def expand_slots(adapter_table, blocks):
    return jnp.einsum(
        "ob,brf->orf", adapter_table, blocks, preferred_element_type=jnp.float32
    ).astype(jnp.bfloat16)


def gather_slot_rows(adapter_table, slots):
    gathered = jnp.einsum(
        "ob,orf->brf", adapter_table, slots, preferred_element_type=jnp.float32
    ).astype(jnp.bfloat16)
    return gathered.reshape(gathered.shape[0] * gathered.shape[1], gathered.shape[2])


def pick_factor(slot_hot, factor):
    return jnp.einsum("se,ekf->skf", slot_hot, factor, preferred_element_type=jnp.float32).astype(
        jnp.bfloat16
    )


def lower_rank(blocks, factor):
    return jnp.einsum("srf,skf->srk", blocks, factor, preferred_element_type=jnp.float32)


def raise_rank(ranks, factor):
    lifted_rows = jnp.einsum("srk,skf->srf", ranks, factor, preferred_element_type=jnp.float32)
    return (adapter_scale * lifted_rows).astype(jnp.bfloat16)


def factor_gradient(ranks, blocks, slot_weights):
    per_slot = jnp.einsum("srk,srf->skf", ranks, blocks, preferred_element_type=jnp.float32)
    summed_rows = jnp.einsum(
        "se,skf->ekf", slot_weights, per_slot, preferred_element_type=jnp.float32
    )
    return adapter_scale * summed_rows


def transposed(left, right):
    return lax.dot_general(
        left, right, (((1,), (1,)), ((), ())), preferred_element_type=jnp.float32
    )


def on_device(
    hidden,
    attended,
    query_cotangent,
    output_cotangent,
    query_projection_weight,
    output_projection_weight,
    narrower,
    widener,
    reducer,
    enlarger,
    block_adapter,
    block_fill,
):
    tokens = hidden.shape[0]
    group_blocks = block_adapter.shape[0]
    width = tokens // group_blocks
    owners = lax.axis_size("dp")
    capacity = -(-group_blocks // owners)
    per_owner = narrower.shape[0]
    owner_of = block_adapter // per_owner
    later_ids = lax.broadcasted_iota(jnp.int32, (group_blocks, group_blocks), 0)
    earlier_ids = lax.broadcasted_iota(jnp.int32, (group_blocks, group_blocks), 1)
    before = (owner_of[:, None] == owner_of[None, :]) & (earlier_ids < later_ids)
    position = jnp.sum(before.astype(jnp.int32), axis=1)
    slot_of = owner_of * capacity + position
    slot_ids = lax.broadcasted_iota(jnp.int32, (owners * capacity, group_blocks), 0)
    adapter_table = (slot_ids == slot_of[None, :]).astype(jnp.bfloat16)
    local_ids = lax.broadcasted_iota(jnp.int32, (group_blocks, per_owner), 1)
    local_hot = (local_ids == (block_adapter % per_owner)[:, None]).astype(jnp.bfloat16)
    slot_hot = jnp.dot(adapter_table, local_hot, preferred_element_type=jnp.float32).astype(
        jnp.bfloat16
    )
    row_ids = lax.broadcasted_iota(jnp.int32, (group_blocks, width), 1)
    live = (row_ids < block_fill[:, None]).astype(jnp.bfloat16).reshape(tokens, 1)
    query_masked = query_cotangent * live
    output_masked = output_cotangent * live

    def to_blocks(values):
        return values.reshape(group_blocks, width, values.shape[1])

    hid_full, att_full = side_by_side((hidden, attended), "mp", 1, 0)
    query_columns, output_columns = side_by_side(
        (query_projection_weight, output_projection_weight), "dp", 0, 1
    )
    query_base_product = jnp.dot(hid_full, query_columns, preferred_element_type=jnp.float32)
    output_base_product = jnp.dot(att_full, output_columns, preferred_element_type=jnp.float32)
    hidden_part = transposed(query_masked, query_columns)
    attended_part = transposed(output_masked, output_columns)
    hidden_total_sum, attended_total_sum = tuple(
        (
            part.astype(jnp.float32)
            for part in in_one_piece(
                (hidden_part.astype(jnp.bfloat16), attended_part.astype(jnp.bfloat16)), "mp", 1, 0
            )
        )
    )
    hid_send = expand_slots(adapter_table, to_blocks(hidden))
    att_send = expand_slots(adapter_table, to_blocks(attended))
    qcot_send = expand_slots(adapter_table, to_blocks(query_masked))
    ocot_send = expand_slots(adapter_table, to_blocks(output_masked))
    hid_recv, att_recv, hot_recv = sent_together((hid_send, att_send, slot_hot), "dp", 0, 0, 1)
    query_down_factor = pick_factor(hot_recv, narrower)
    query_up_factor = pick_factor(hot_recv, widener)
    output_down_factor = pick_factor(hot_recv, reducer)
    output_up_factor = pick_factor(hot_recv, enlarger)
    query_rank_rows, output_rank_rows = (
        of_everyone(lower_rank(hid_recv, query_down_factor).astype(jnp.bfloat16), "mp").astype(
            jnp.float32
        ),
        of_everyone(lower_rank(att_recv, output_down_factor).astype(jnp.bfloat16), "mp").astype(
            jnp.float32
        ),
    )
    query_rank_rows = query_rank_rows.astype(jnp.bfloat16)
    output_rank_rows = output_rank_rows.astype(jnp.bfloat16)
    query_slot_rows, output_slot_rows = sent_together_2(
        (
            raise_rank(query_rank_rows, query_up_factor),
            raise_rank(output_rank_rows, output_up_factor),
        ),
        "dp",
        0,
        0,
        1,
    )
    qcot_recv, ocot_recv = sent_together_2((qcot_send, ocot_send), "dp", 0, 0, 1)
    query_backward_pass, output_backward_pass = (
        of_everyone(lower_rank(qcot_recv, query_up_factor).astype(jnp.bfloat16), "mp").astype(
            jnp.float32
        ),
        of_everyone(lower_rank(ocot_recv, output_up_factor).astype(jnp.bfloat16), "mp").astype(
            jnp.float32
        ),
    )
    query_backward_pass = query_backward_pass.astype(jnp.bfloat16)
    output_backward_pass = output_backward_pass.astype(jnp.bfloat16)
    hidden_slot_rows, attended_slot_rows = sent_together_2(
        (
            raise_rank(query_backward_pass, query_down_factor),
            raise_rank(output_backward_pass, output_down_factor),
        ),
        "dp",
        0,
        0,
        1,
    )
    slot_weights = hot_recv.astype(jnp.float32)
    narrower_gradient = factor_gradient(query_backward_pass, hid_recv, slot_weights)
    widener_gradient = factor_gradient(query_rank_rows, qcot_recv, slot_weights)
    reducer_gradient = factor_gradient(output_backward_pass, att_recv, slot_weights)
    enlarger_gradient = factor_gradient(output_rank_rows, ocot_recv, slot_weights)
    query_adapter_term = gather_slot_rows(adapter_table, query_slot_rows)
    output_adapter_term = gather_slot_rows(adapter_table, output_slot_rows)
    hidden_adapter_term = gather_slot_rows(adapter_table, hidden_slot_rows)
    attended_adapter_term = gather_slot_rows(adapter_table, attended_slot_rows)
    queries = (query_base_product + query_adapter_term.astype(jnp.float32)).astype(jnp.bfloat16)
    projected = (output_base_product + output_adapter_term.astype(jnp.float32)).astype(jnp.bfloat16)
    hidden_state_gradient = (hidden_total_sum + hidden_adapter_term.astype(jnp.float32)).astype(
        jnp.bfloat16
    )
    attention_output_gradient = (
        attended_total_sum + attended_adapter_term.astype(jnp.float32)
    ).astype(jnp.bfloat16)
    return (
        queries,
        projected,
        hidden_state_gradient,
        attention_output_gradient,
        narrower_gradient,
        widener_gradient,
        reducer_gradient,
        enlarger_gradient,
    )


def solution(mesh):
    placed = (
        P("dp", "mp"),
        P("dp", "mp"),
        P("dp", "mp"),
        P("dp", "mp"),
        P("dp", "mp"),
        P("dp", "mp"),
        P("dp", None, "mp"),
        P("dp", None, "mp"),
        P("dp", None, "mp"),
        P("dp", None, "mp"),
        P("dp"),
        P("dp"),
    )
    return jax.shard_map(
        on_device,
        mesh=mesh,
        in_specs=placed,
        out_specs=(
            P("dp", "mp"),
            P("dp", "mp"),
            P("dp", "mp"),
            P("dp", "mp"),
            P("dp", None, "mp"),
            P("dp", None, "mp"),
            P("dp", None, "mp"),
            P("dp", None, "mp"),
        ),
        check_vma=False,
    )
```

profile of v0, /device:TPU:16, one launch (start us, length us, event | category | flops | bytes accessed | tf_op | source)
XLA Modules:
  0.0 211.6 jit_solution(4963414512849389488)
XLA Ops:
  15.4 16.5 %all-to-all-start = ((bf16[64,2,2056]{2,1,0:T(2,128)(2,1)}), bf16[64,2,2056]{2,1,0:T(2,128)(2,1)S(1)}, u32[]{:S(2)}, u32[]{:S(2)}) async-start(bf16[64,2,2056]{2,1,0:T(2,128)(2,1)} %reshape.92), calls=%async_computation | async-start | bytes 1114112 | tf_op jit(solution)/shard_map/all_to_all | solution.py:34
  35.0 18.4 %all-to-all-done = bf16[64,2,2056]{2,1,0:T(2,128)(2,1)S(1)} async-done(((bf16[64,2,2056]{2,1,0:T(2,128)(2,1)}), bf16[64,2,2056]{2,1,0:T(2,128)(2,1)S(1)}, u32[]{:S(2)}, u32[]{:S(2)}) %all-to-all-start) | async-done | bytes 526368 | tf_op jit(solution)/shard_map/all_to_all | solution.py:34
  53.4 6.0 %all-to-all-start.4 = ((bf16[64,8,512]{2,1,0:T(8,128)(2,1)}), bf16[64,8,512]{2,1,0:T(8,128)(2,1)S(1)}, u32[]{:S(2)}, u32[]{:S(2)}) async-start(bf16[64,8,512]{2,1,0:T(8,128)(2,1)} %copy.215), calls=%async_computation.5 | async-start | bytes 1048576 | tf_op jit(solution)/shard_map/all_to_all | solution.py:59
  69.8 2.4 %convolution_convert_fusion.2 = bf16[64,16,512]{2,0,1:T(8,128)(2,1)} fusion(bf16[16,16,512]{2,1,0:T(8,128)(2,1)} %param.21, bf16[64,4112]{0,1:T(8,128)(2,1)S(1)} %bitcast.64), kind=kOutput, calls=%fused_computation.17 | convolution fusion | flops 17301504 | bytes 1314816 | tf_op jit(solution)/shard_map/se,ekf->skf/dot_general | solution.py:80
  73.7 4.9 %all-to-all-done.4 = bf16[64,8,512]{2,1,0:T(8,128)(2,1)S(1)} async-done(((bf16[64,8,512]{2,1,0:T(8,128)(2,1)}), bf16[64,8,512]{2,1,0:T(8,128)(2,1)S(1)}, u32[]{:S(2)}, u32[]{:S(2)}) %all-to-all-start.4) | async-done | bytes 524320 | tf_op jit(solution)/shard_map/all_to_all | solution.py:59
  78.7 4.4 %all-to-all-start.2 = ((bf16[8,2,2048]{2,1,0:T(2,128)(2,1)}), bf16[8,2,2048]{2,1,0:T(2,128)(2,1)}, u32[]{:S(2)}, u32[]{:S(2)}) async-start(bf16[8,2,2048]{2,1,0:T(2,128)(2,1)} %reshape.94), calls=%async_computation.2 | async-start | bytes 131072 | tf_op jit(solution)/shard_map/all_to_all | solution.py:43
  83.1 2.1 convolution_convert_fusion.14
  90.3 4.8 %all-to-all-start.1 = ((bf16[8,2,2048]{2,1,0:T(2,128)(2,1)}), bf16[8,2,2048]{2,1,0:T(2,128)(2,1)}, u32[]{:S(2)}, u32[]{:S(2)}) async-start(bf16[8,2,2048]{2,1,0:T(2,128)(2,1)} %reshape.96), calls=%async_computation.1 | async-start | bytes 131072 | tf_op jit(solution)/shard_map/all_to_all | solution.py:43
  98.4 2.4 %all-to-all-done.1 = bf16[8,2,2048]{2,1,0:T(2,128)(2,1)} async-done(((bf16[8,2,2048]{2,1,0:T(2,128)(2,1)}), bf16[8,2,2048]{2,1,0:T(2,128)(2,1)}, u32[]{:S(2)}, u32[]{:S(2)}) %all-to-all-start.1) | async-done | bytes 65568 | tf_op jit(solution)/shard_map/all_to_all | solution.py:43
  100.8 4.0 %all-to-all-start.6 = ((bf16[8,2,2048]{2,1,0:T(2,128)(2,1)}), bf16[8,2,2048]{2,1,0:T(2,128)(2,1)}, u32[]{:S(2)}, u32[]{:S(2)}) async-start(bf16[8,2,2048]{2,1,0:T(2,128)(2,1)} %reshape.98), calls=%async_computation.7 | async-start | bytes 131072 | tf_op jit(solution)/shard_map/all_to_all | solution.py:43
  108.0 2.4 %all-to-all-done.6 = bf16[8,2,2048]{2,1,0:T(2,128)(2,1)} async-done(((bf16[8,2,2048]{2,1,0:T(2,128)(2,1)}), bf16[8,2,2048]{2,1,0:T(2,128)(2,1)}, u32[]{:S(2)}, u32[]{:S(2)}) %all-to-all-start.6) | async-done | bytes 65568 | tf_op jit(solution)/shard_map/all_to_all | solution.py:43
  110.4 3.5 %all-to-all-start.5 = ((bf16[8,2,2048]{2,1,0:T(2,128)(2,1)}), bf16[8,2,2048]{2,1,0:T(2,128)(2,1)S(1)}, u32[]{:S(2)}, u32[]{:S(2)}) async-start(bf16[8,2,2048]{2,1,0:T(2,128)(2,1)} %reshape.100), calls=%async_computation.6 | async-start | bytes 131072 | tf_op jit(solution)/shard_map/all_to_all | solution.py:43
  114.9 2.0 fusion.27
  116.9 2.0 fusion.26
  121.4 8.0 %all-to-all-start.3 = ((bf16[64,8,512]{2,1,0:T(8,128)(2,1)}), bf16[64,8,512]{2,1,0:T(8,128)(2,1)}, u32[]{:S(2)}, u32[]{:S(2)}) async-start(bf16[64,8,512]{2,1,0:T(8,128)(2,1)} %pad_maximum_fusion.1), calls=%async_computation.3 | async-start | bytes 1048576 | tf_op jit(solution)/shard_map/all_to_all | solution.py:59
  132.9 1.9 fusion.29
  134.9 3.7 %convolution_convert_fusion = bf16[128,4096]{1,0:T(8,128)(2,1)S(1)} fusion(bf16[128,512]{1,0:T(8,128)(2,1)S(1)} %copy-done.8, bf16[4096,1024]{1,0:T(8,128)(2,1)} %all-gather.5.cloned.1.call-done), kind=kOutput, calls=%fused_computation | convolution fusion | flops 537395200 | bytes 5373952 | tf_op jit(solution)/shard_map/dot_general | solution.py:103
  138.6 3.7 %convolution_convert_fusion.1 = bf16[128,4096]{1,0:T(8,128)(2,1)S(1)} fusion(bf16[128,512]{1,0:T(8,128)(2,1)S(1)} %get-tuple-element.56, bf16[4096,1024]{1,0:T(8,128)(2,1)} %all-gather.5.cloned.1.call-done), kind=kOutput, calls=%fused_computation.1 | convolution fusion | flops 537395200 | bytes 5373952 | tf_op jit(solution)/shard_map/dot_general | solution.py:103
  148.0 2.0 fusion.17
  151.5 13.0 %all-to-all-start.7 = ((bf16[64,8,512]{2,1,0:T(8,128)(2,1)}), bf16[64,8,512]{2,1,0:T(8,128)(2,1)}, u32[]{:S(2)}, u32[]{:S(2)}) async-start(bf16[64,8,512]{2,1,0:T(8,128)(2,1)} %pad_maximum_fusion.3), calls=%async_computation.8 | async-start | bytes 1048576 | tf_op jit(solution)/shard_map/all_to_all | solution.py:59
  173.9 9.8 %all-to-all-done.7 = bf16[64,8,512]{2,1,0:T(8,128)(2,1)} async-done(((bf16[64,8,512]{2,1,0:T(8,128)(2,1)}), bf16[64,8,512]{2,1,0:T(8,128)(2,1)}, u32[]{:S(2)}, u32[]{:S(2)}) %all-to-all-start.7) | async-done | bytes 524320 | tf_op jit(solution)/shard_map/all_to_all | solution.py:59
  186.2 4.0 %fusion.41 = bf16[128,512]{1,0:T(8,128)(2,1)} fusion(f32[128,512]{1,0:T(8,128)S(1)} %reshape.85, bf16[4096,1024]{1,0:T(8,128)(2,1)} %all-gather.5.cloned.1.call-done, bf16[256,4096]{1,0:T(8,128)(2,1)} %all-gather.3.cloned.1.call-done), kind=kOutput, calls=%fused_computation.42 | convolution fusion | flops 537001984 | bytes 5636096 | tf_op jit(solution)/shard_map/dot_general | solution.py:153
  190.3 3.6 %fusion.38 = bf16[128,512]{1,0:T(8,128)(2,1)} fusion(f32[128,512]{1,0:T(8,128)S(1)} %reshape.86, bf16[4096,1024]{1,0:T(8,128)(2,1)} %all-gather.5.cloned.1.call-done, bf16[256,4096]{1,0:T(8,128)(2,1)S(1)} %copy-done.22), kind=kOutput, calls=%fused_computation.41 | convolution fusion | flops 537001984 | bytes 5636096 | tf_op jit(solution)/shard_map/dot_general | solution.py:154
  193.9 9.4 %reduce-scatter.2.cloned.1.call-done = bf16[256,512]{1,0:T(8,128)(2,1)} async-done(((bf16[256,4096]{1,0:T(8,128)(2,1)}), bf16[256,512]{1,0:T(8,128)(2,1)}) %reduce-scatter.2.cloned.1.call-update) | async-done | bytes 262160 | tf_op jit(solution)/shard_map/reduce_scatter | solution.py:22
  (148 shorter events, 62.3 us)
Async XLA Ops:
  7.2 54.9 %copy-start = (bf16[16,16,512]{2,1,0:T(8,128)(2,1)S(1)}, bf16[16,16,512]{2,1,0:T(8,128)(2,1)}, u32[]{:S(2)}) copy-start(bf16[16,16,512]{2,1,0:T(8,128)(2,1)} %param.20) | copy-start | bytes 786436
  7.2 127.7 %all-gather.5.cloned.1.call-start = ((), (), s32[]{:S(2)}) async-start(), calls=%async_computation.10 | async-start | bytes 8519680 | tf_op jit(solution)/shard_map/all_gather | solution.py:13
  12.7 19.3 %copy-start.9 = (bf16[128,512]{1,0:T(8,128)(2,1)S(1)}, bf16[128,512]{1,0:T(8,128)(2,1)}, u32[]{:S(2)}) copy-start(bf16[128,512]{1,0:T(8,128)(2,1)} %param.13) | copy-start | bytes 393220
  12.7 19.3 %copy-start.10 = (bf16[128,512]{1,0:T(8,128)(2,1)S(1)}, bf16[128,512]{1,0:T(8,128)(2,1)}, u32[]{:S(2)}) copy-start(bf16[128,512]{1,0:T(8,128)(2,1)} %param.12) | copy-start | bytes 393220
  12.8 20.0 %copy-start.21 = (s32[32]{0:T(128)S(1)}, s32[32]{0:T(128)}, u32[]{:S(2)}) copy-start(s32[32]{0:T(128)} %param.23) | copy-start | bytes 388
  12.8 20.2 %copy-start.17 = (bf16[128,512]{1,0:T(8,128)(2,1)S(1)}, bf16[128,512]{1,0:T(8,128)(2,1)}, u32[]{:S(2)}) copy-start(bf16[128,512]{1,0:T(8,128)(2,1)} %param.14) | copy-start | bytes 393220
  12.8 20.2 %copy-start.18 = (bf16[128,512]{1,0:T(8,128)(2,1)S(1)}, bf16[128,512]{1,0:T(8,128)(2,1)}, u32[]{:S(2)}) copy-start(bf16[128,512]{1,0:T(8,128)(2,1)} %param.15) | copy-start | bytes 393220
  15.4 38.0 %all-to-all-start = ((bf16[64,2,2056]{2,1,0:T(2,128)(2,1)}), bf16[64,2,2056]{2,1,0:T(2,128)(2,1)S(1)}, u32[]{:S(2)}, u32[]{:S(2)}) async-start(bf16[64,2,2056]{2,1,0:T(2,128)(2,1)} %reshape.92), calls=%async_computation | async-start | bytes 1114112 | tf_op jit(solution)/shard_map/all_to_all | solution.py:34
  31.9 154.3 %all-gather.3.cloned.1.call-start = ((), (), s32[]{:S(2)}) async-start(), calls=%async_computation.9 | async-start | bytes 2359296 | tf_op jit(solution)/shard_map/all_gather | solution.py:13
  33.0 20.4 %copy-start.7 = (bf16[128,512]{1,0:T(8,128)(2,1)}, bf16[128,512]{1,0:T(8,128)(2,1)S(1)}, u32[]{:S(2)}) copy-start(bf16[128,512]{1,0:T(8,128)(2,1)S(1)} %get-tuple-element.57) | copy-start | bytes 393220
  53.4 25.3 %all-to-all-start.4 = ((bf16[64,8,512]{2,1,0:T(8,128)(2,1)}), bf16[64,8,512]{2,1,0:T(8,128)(2,1)S(1)}, u32[]{:S(2)}, u32[]{:S(2)}) async-start(bf16[64,8,512]{2,1,0:T(8,128)(2,1)} %copy.215), calls=%async_computation.5 | async-start | bytes 1048576 | tf_op jit(solution)/shard_map/all_to_all | solution.py:59
  66.9 5.3 %copy-start.11 = (bf16[16,16,512]{2,1,0:T(8,128)(2,1)S(1)}, bf16[16,16,512]{2,1,0:T(8,128)(2,1)}, u32[]{:S(2)}) copy-start(bf16[16,16,512]{2,1,0:T(8,128)(2,1)} %param.19) | copy-start | bytes 786436
  78.7 11.6 %all-to-all-start.2 = ((bf16[8,2,2048]{2,1,0:T(2,128)(2,1)}), bf16[8,2,2048]{2,1,0:T(2,128)(2,1)}, u32[]{:S(2)}, u32[]{:S(2)}) async-start(bf16[8,2,2048]{2,1,0:T(2,128)(2,1)} %reshape.94), calls=%async_computation.2 | async-start | bytes 131072 | tf_op jit(solution)/shard_map/all_to_all | solution.py:43
  90.3 10.5 %all-to-all-start.1 = ((bf16[8,2,2048]{2,1,0:T(2,128)(2,1)}), bf16[8,2,2048]{2,1,0:T(2,128)(2,1)}, u32[]{:S(2)}, u32[]{:S(2)}) async-start(bf16[8,2,2048]{2,1,0:T(2,128)(2,1)} %reshape.96), calls=%async_computation.1 | async-start | bytes 131072 | tf_op jit(solution)/shard_map/all_to_all | solution.py:43
  100.8 9.6 %all-to-all-start.6 = ((bf16[8,2,2048]{2,1,0:T(2,128)(2,1)}), bf16[8,2,2048]{2,1,0:T(2,128)(2,1)}, u32[]{:S(2)}, u32[]{:S(2)}) async-start(bf16[8,2,2048]{2,1,0:T(2,128)(2,1)} %reshape.98), calls=%async_computation.7 | async-start | bytes 131072 | tf_op jit(solution)/shard_map/all_to_all | solution.py:43
  108.0 11.9 %copy-start.12 = (bf16[64,4,16]{2,1,0:T(4,128)(2,1)}, bf16[64,4,16]{2,1,0:T(4,128)(2,1)S(1)}, u32[]{:S(2)}) copy-start(bf16[64,4,16]{2,1,0:T(4,128)(2,1)S(1)} %copy.200) | copy-start | bytes 24580
  110.4 11.0 %all-to-all-start.5 = ((bf16[8,2,2048]{2,1,0:T(2,128)(2,1)}), bf16[8,2,2048]{2,1,0:T(2,128)(2,1)S(1)}, u32[]{:S(2)}, u32[]{:S(2)}) async-start(bf16[8,2,2048]{2,1,0:T(2,128)(2,1)} %reshape.100), calls=%async_computation.6 | async-start | bytes 131072 | tf_op jit(solution)/shard_map/all_to_all | solution.py:43
  121.4 11.6 %copy-start.15 = (bf16[64,4,16]{2,1,0:T(4,128)(2,1)}, bf16[64,4,16]{2,1,0:T(4,128)(2,1)S(1)}, u32[]{:S(2)}) copy-start(bf16[64,4,16]{2,1,0:T(4,128)(2,1)S(1)} %copy.222) | copy-start | bytes 24580
  121.4 30.1 %all-to-all-start.3 = ((bf16[64,8,512]{2,1,0:T(8,128)(2,1)}), bf16[64,8,512]{2,1,0:T(8,128)(2,1)}, u32[]{:S(2)}, u32[]{:S(2)}) async-start(bf16[64,8,512]{2,1,0:T(8,128)(2,1)} %pad_maximum_fusion.1), calls=%async_computation.3 | async-start | bytes 1048576 | tf_op jit(solution)/shard_map/all_to_all | solution.py:59
  129.4 73.9 %reduce-scatter.2.cloned.1.call-start = ((), (), s32[]{:S(2)}) async-start(), calls=%async_computation.11 | async-start | bytes 2359296 | tf_op jit(solution)/shard_map/reduce_scatter | solution.py:22
  151.5 15.4 %copy-start.1 = (f32[16,16,512]{2,0,1:T(8,128)S(1)}, f32[16,16,512]{2,0,1:T(8,128)}, u32[]{:S(2)}) copy-start(f32[16,16,512]{2,0,1:T(8,128)} %fusion.17) | copy-start | bytes 1572868
  151.5 32.1 %all-to-all-start.7 = ((bf16[64,8,512]{2,1,0:T(8,128)(2,1)}), bf16[64,8,512]{2,1,0:T(8,128)(2,1)}, u32[]{:S(2)}, u32[]{:S(2)}) async-start(bf16[64,8,512]{2,1,0:T(8,128)(2,1)} %pad_maximum_fusion.3), calls=%async_computation.8 | async-start | bytes 1048576 | tf_op jit(solution)/shard_map/all_to_all | solution.py:59
  164.6 4.5 %copy-start.4 = (bf16[64,16,512]{2,1,0:T(8,128)(2,1)S(1)}, bf16[64,16,512]{2,1,0:T(8,128)(2,1)}, u32[]{:S(2)}) copy-start(bf16[64,16,512]{2,1,0:T(8,128)(2,1)} %fusion.66) | copy-start | bytes 3145732
  186.2 4.1 %copy-start.22 = (bf16[256,4096]{1,0:T(8,128)(2,1)S(1)}, bf16[256,4096]{1,0:T(8,128)(2,1)}, u32[]{:S(2)}) copy-start(bf16[256,4096]{1,0:T(8,128)(2,1)} %all-gather.3.cloned.1.call-done) | copy-start | bytes 6291460
  (10 other events, 26.1 us)
Sparse Core Ops, SparseCore 0:
  11.6 118.1 all-gather.4
  131.9 28.7 all-gather.2
  163.5 39.7 reduce-scatter.1
where the time goes:
time: 213 us; the launch traced here: 212 us
  starting transfers between devices  60.3 us (28%)
  waiting for transfers between devices  47.5 us (22%)
  matrix products  44.6 us (21%)
  local copies, waits for them, and re-layouts  33.1 us (16%)
  between operations  14.4 us (7%)
  other arithmetic  11.6 us (5%)
    all_to_all x3, starting transfers between devices, sent_together_2(): lax.all_to_all(both, axis, split_axis=split_dim, concat_axis=concat_dim,...  27 us
    all_to_all x1, waiting for transfers between devices, sent_together(): lax.all_to_all(both, axis, split_axis=split_dim, concat_axis=concat_dim,...  18.4 us
    all_to_all x4, starting transfers between devices, copy_for_each(): return lax.all_to_all(copies, axis, split_axis=0, concat_axis=0, tiled=True)  16.7 us
    all_to_all x1, starting transfers between devices, sent_together(): lax.all_to_all(both, axis, split_axis=split_dim, concat_axis=concat_dim,...  16.5 us
    unnamed x64, local copies, waits for them, and re-layouts  16 us
    all_to_all x3, waiting for transfers between devices, sent_together_2(): lax.all_to_all(both, axis, split_axis=split_dim, concat_axis=concat_dim,...  14.8 us
    reduce_scatter x1, waiting for transfers between devices, in_one_piece(): lax.psum_scatter(both, axis, scatter_dimension=dim, tiled=True)  9.42 us
    dot_general x2, matrix products, transposed(): lax.dot_general(left, right, (((1,), (1,)), ((), ())), preferred_element_...  7.34 us
  transfers between devices with their start and end apart: 11, of which 6 were waited for; matrix products, arithmetic and copies ran while one was open for 40% of the time, Pallas kernels for 0%

commit v1 on v0

v1 whole, which is shorter than its diff:
```python
import jax
import jax.numpy as jnp
from jax import lax
from jax.experimental import pallas as pl
from jax.experimental.pallas import tpu as pltpu
from jax.sharding import Mesh
from jax.sharding import PartitionSpec as P

adapter_scale = 2.0
F32 = jnp.float32
BF16 = jnp.bfloat16
DP = ("y", "z")
MP = ("x", "c")


def matmul(left, right, ldim=1, rdim=0):
    return lax.dot_general(
        left, right, (((ldim,), (rdim,)), ((), ())), preferred_element_type=F32
    )


def iota(shape, dim):
    return lax.broadcasted_iota(jnp.int32, shape, dim)


def forward_kernel(order_ref, *refs):
    row_refs, (w_ref, keep_ref, give_ref, total) = refs[:-4], refs[-4:]
    step = pl.program_id(0)
    sides, tokens, width = keep_ref.shape

    @pl.when(step == 0)
    def _():
        total[...] = jnp.zeros_like(total)

    for k, rows_ref in enumerate(row_refs):

        @pl.when(step == k)
        def _():
            for w in range(sides):
                rows = jnp.concatenate([rows_ref[0, w], rows_ref[1, w]], axis=0)
                total[w] += jnp.dot(
                    rows, w_ref[0, :, w * width : (w + 1) * width], preferred_element_type=F32
                )

    @pl.when(step == pl.num_programs(0) - 1)
    def _():
        keep_ref[...] = total[:, :tokens]
        give_ref[...] = total[:, tokens:].astype(BF16)


def forward_base(order, rows, weights):
    steps, depth, wide = weights.shape
    _, sides, tokens, _ = rows[0].shape
    width = wide // sides
    whole = pl.BlockSpec(rows[0].shape, lambda k, order: (0, 0, 0, 0))
    out = pl.BlockSpec((sides, tokens, width), lambda k, order: (0, 0, 0))
    return pl.pallas_call(
        forward_kernel,
        grid_spec=pltpu.PrefetchScalarGridSpec(
            num_scalar_prefetch=1,
            grid=(steps,),
            in_specs=[whole] * steps
            + [pl.BlockSpec((1, depth, wide), lambda k, order: (order[k], 0, 0))],
            out_specs=[out, out],
            scratch_shapes=[pltpu.VMEM((sides, 2 * tokens, width), F32)],
        ),
        out_shape=[
            jax.ShapeDtypeStruct((sides, tokens, width), F32),
            jax.ShapeDtypeStruct((sides, tokens, width), BF16),
        ],
        compiler_params=pltpu.CompilerParams(dimension_semantics=("arbitrary",)),
        cost_estimate=pl.CostEstimate(
            flops=4 * tokens * steps * depth * wide,
            bytes_accessed=weights.size * 2 + 2 * steps * rows[0].size,
            transcendentals=0,
        ),
        name="forward_base",
    )(order, *rows, weights)


def backward_kernel(first_ref, own_ref, other_ref, w_ref, out_ref, part):
    sides, tokens, width = own_ref.shape
    for w in range(sides):
        rows = jnp.concatenate([own_ref[w], other_ref[w]], axis=0)
        part[w] = lax.dot_general(
            rows,
            w_ref[0, :, w * width : (w + 1) * width],
            (((1,), (1,)), ((), ())),
            preferred_element_type=F32,
        )
    own_first = first_ref[0] == 0

    @pl.when(own_first)
    def _():
        out_ref[0, 0] = part[:, :tokens].astype(BF16)
        out_ref[0, 1] = part[:, tokens:].astype(BF16)

    @pl.when(jnp.logical_not(own_first))
    def _():
        out_ref[0, 0] = part[:, tokens:].astype(BF16)
        out_ref[0, 1] = part[:, :tokens].astype(BF16)


def backward_base(first, own, other, weights):
    steps, depth, wide = weights.shape
    sides, tokens, _ = own.shape
    width = wide // sides
    rows = pl.BlockSpec((sides, tokens, width), lambda k, first: (0, 0, 1))
    out = pl.BlockSpec((1, 2, sides, tokens, depth), lambda k, first: (k, 0, 0, 0, 0))
    return pl.pallas_call(
        backward_kernel,
        grid_spec=pltpu.PrefetchScalarGridSpec(
            num_scalar_prefetch=1,
            grid=(steps,),
            in_specs=[rows, rows, pl.BlockSpec((1, depth, wide), lambda k, first: (k, 0, 0))],
            out_specs=out,
            scratch_shapes=[pltpu.VMEM((sides, 2 * tokens, depth), F32)],
        ),
        out_shape=jax.ShapeDtypeStruct((steps, 2, sides, tokens, depth), BF16),
        compiler_params=pltpu.CompilerParams(dimension_semantics=("arbitrary",)),
        cost_estimate=pl.CostEstimate(
            flops=4 * tokens * steps * depth * wide,
            bytes_accessed=weights.size * 2 + 4 * steps * sides * tokens * depth,
            transcendentals=0,
        ),
        name="backward_base",
    )(first, own, other, weights)


def on_device(
    hidden,
    attended,
    query_cotangent,
    output_cotangent,
    query_projection_weight,
    output_projection_weight,
    narrower,
    widener,
    reducer,
    enlarger,
    block_adapter,
    block_fill,
):
    tokens, width = hidden.shape
    blocks = block_adapter.shape[0]
    rows = tokens // blocks
    ny, nx, nc = lax.axis_size("y"), lax.axis_size("x"), lax.axis_size("c")
    owners = ny * lax.axis_size("z")
    mine, rank = narrower.shape[:2]
    y, x, c = lax.axis_index("y"), lax.axis_index("x"), lax.axis_index("c")
    odd = y % 2
    neighbour = [(i, i ^ 1) for i in range(ny)]

    weights = jnp.concatenate([query_projection_weight, output_projection_weight], axis=1)
    same_parity = [[p + 2 * i for i in range(ny // 2)] for p in range(2)]
    weights = lax.all_gather(weights, "y", axis=0, axis_index_groups=same_parity)
    weights = lax.all_gather(weights, "z", axis=1, tiled=True)

    owner_of = (block_adapter // mine).astype(BF16)
    local_of = block_adapter % mine
    fill = block_fill.astype(BF16)
    in_block = (iota((tokens, blocks), 0) // rows == iota((tokens, blocks), 1)).astype(BF16)
    local_hot = (iota((blocks, 128), 1) == local_of[:, None]).astype(BF16)
    token_local = matmul(in_block, local_hot).astype(BF16)
    token_fill = matmul(in_block, jnp.broadcast_to(fill[:, None], (blocks, 128)))[:, :1]
    live = (iota((tokens, 1), 0) % rows < token_fill.astype(jnp.int32)).astype(BF16)
    token_owner = matmul(jnp.broadcast_to(owner_of[None, :], (8, blocks)), in_block, 1, 1)[:1]
    token_owner = token_owner.astype(jnp.int32)
    both = 2 * tokens
    slot_rows = owners * 2 * rows
    table_owner = jnp.concatenate([token_owner, token_owner], axis=1)
    table_row = iota((slot_rows, both), 0)
    table_col = iota((slot_rows, both), 1)
    table = (
        (table_row // (2 * rows) == table_owner)
        & (table_row % rows == table_col % rows)
        & ((table_row // rows) % 2 == table_col // tokens)
    ).astype(BF16)

    inputs = jnp.concatenate([hidden, attended], axis=0)
    cotangents = jnp.concatenate([query_cotangent * live, output_cotangent * live], axis=0)

    tags = jnp.concatenate([token_local, token_local], axis=0)
    payload = jnp.concatenate([inputs, cotangents, tags], axis=1)

    other = lax.ppermute(payload, "y", neighbour)
    at_home = c == odd
    hand_over = [(a * nc + a % 2, a * nc + 1 - a % 2) for a in range(ny)]
    trade = [
        (a * nc + b, ((a ^ 1) * nc + (b ^ 1)) if a % 2 != b else a * nc + b)
        for a in range(ny)
        for b in range(nc)
    ]
    features = jnp.concatenate([payload[:, :width], other[:, :width]], axis=0)
    features = jnp.where(at_home, features, lax.ppermute(features, ("y", "c"), hand_over))
    shifts = (0, 1, nx - 1, 2)
    order = jnp.stack([(x + nx - k) % nx for k in shifts]).astype(jnp.int32)
    gathered = [features]
    for k in shifts[1:]:
        ring = [(i, (i + k) % nx) for i in range(nx)]
        gathered.append(lax.ppermute(features, "x", ring))
    features = [f.reshape(2, 2, tokens, width) for f in gathered]

    send = matmul(table, payload).astype(BF16).reshape(owners, 2 * rows, payload.shape[1])
    recv = lax.all_to_all(send, DP, 0, 0, tiled=True).reshape(slot_rows, payload.shape[1])
    slot_inputs = recv[:, :width]
    slot_cotangents = recv[:, width : 2 * width]
    slot_tags = recv[:, 2 * width :]
    lanes = 2 * mine * rank
    half = mine * rank
    spread = (iota((128, lanes), 0) == (iota((128, lanes), 1) % half) // rank).astype(BF16)
    side = (iota((slot_rows, lanes), 0) // rows) % 2 == iota((slot_rows, lanes), 1) // half
    mask = matmul(slot_tags, spread).astype(BF16) * side.astype(BF16)
    fold = (iota((lanes, rank), 0) % rank == iota((lanes, rank), 1)).astype(BF16)
    down = jnp.concatenate([narrower.reshape(half, width), reducer.reshape(half, width)], axis=0)
    up = jnp.concatenate([widener.reshape(half, width), enlarger.reshape(half, width)], axis=0)
    forward_wide = matmul(slot_inputs, down, 1, 1).astype(BF16) * mask
    backward_wide = matmul(slot_cotangents, up, 1, 1).astype(BF16) * mask
    forward_part = matmul(fold, forward_wide, 0, 1).astype(BF16)
    backward_part = matmul(fold, backward_wide, 0, 1).astype(BF16)
    parts = jnp.concatenate([forward_part, backward_part], axis=0)
    shares = lax.axis_size(MP)
    copies = jnp.broadcast_to(parts, (shares, *parts.shape))
    everyone = lax.all_to_all(copies, MP, 0, 0, tiled=True)
    ranks = jnp.sum(everyone.astype(F32), axis=0).astype(BF16)
    forward_ranks = matmul(ranks[:rank], fold, 0, 1).astype(BF16) * mask
    backward_ranks = matmul(ranks[rank:], fold, 0, 1).astype(BF16) * mask
    raised = jnp.concatenate(
        [
            (adapter_scale * matmul(forward_ranks, up)).astype(BF16),
            (adapter_scale * matmul(backward_ranks, down)).astype(BF16),
        ],
        axis=1,
    )

    def gradient(left, right):
        return (adapter_scale * matmul(left, right, 0, 0)).reshape(mine, rank, width)

    narrower_gradient = gradient(backward_ranks[:, :half], slot_inputs)
    reducer_gradient = gradient(backward_ranks[:, half:], slot_inputs)
    widener_gradient = gradient(forward_ranks[:, :half], slot_cotangents)
    enlarger_gradient = gradient(forward_ranks[:, half:], slot_cotangents)

    gradients = (narrower_gradient, widener_gradient, reducer_gradient, enlarger_gradient)
    raised = raised.reshape(owners, 2 * rows, 2 * width)
    gradients, weights = lax.optimization_barrier((gradients, weights))

    wide = payload.shape[1]
    chunks = backward_base(
        odd.astype(jnp.int32).reshape(1),
        payload.reshape(2, tokens, wide),
        other.reshape(2, tokens, wide),
        weights,
    )
    chunks = chunks.reshape(nx * nc, both, width)
    raised, chunks = lax.optimization_barrier((raised, chunks))
    total = lax.psum_scatter(chunks, MP, scatter_dimension=0, tiled=False)
    total = lax.ppermute(total, ("y", "c"), trade).astype(F32)
    back = lax.all_to_all(
        raised, DP, 0, 0, tiled=True
    ).reshape(slot_rows, 2 * width)
    terms = matmul(table, back, 0, 0)

    keep, give = forward_base(order, features, weights)
    keep = keep.reshape(both, width)
    keep = keep + lax.ppermute(give.reshape(both, width), "y", neighbour).astype(F32)

    forward_out = (keep + terms[:, :width]).astype(BF16)
    backward_out = (total.astype(BF16).astype(F32) + terms[:, width:]).astype(BF16)
    return (
        forward_out[:tokens],
        forward_out[tokens:],
        backward_out[:tokens],
        backward_out[tokens:],
        *gradients,
    )


def solution(mesh):
    grid = Mesh(mesh.devices.reshape(8, 8, 4, 2), ("y", "z", "x", "c"))
    flat = P(DP, MP)
    deep = P(DP, None, MP)

    return jax.shard_map(
        on_device,
        mesh=grid,
        in_specs=(flat,) * 6 + (deep,) * 4 + (P(DP),) * 2,
        out_specs=(flat,) * 4 + (deep,) * 4,
        check_vma=False,
    )
```

time: 213 us -> 198 us (0.930)
  the two profiles are of different devices: /device:TPU:16 before, /device:TPU:1 now
where the time goes in v1:
time: 198 us; the launch traced here: 197 us
  waiting for transfers between devices  73.3 us (37%)
  starting transfers between devices  53.7 us (27%)
  blocking collectives  17.7 us (9%)
  matrix products  16.2 us (8%)
  between operations  14.9 us (8%)
  Pallas kernels  11.4 us (6%)
  local copies, waits for them, and re-layouts  7.04 us (4%)
  other arithmetic  2.35 us (1%)
    all_to_all x1, waiting for transfers between devices, on_device(): lax.all_to_all(send, DP, 0, 0, tiled=True)  25.9 us
    ppermute x3, waiting for transfers between devices, on_device(): gathered.append(lax.ppermute(features, 'x', ring))  25 us
    all_gather x1, blocking collectives, on_device(): lax.all_gather(weights, 'y', axis=0, axis_index_groups=same_parity)  17.7 us
    dot_general x16, matrix products, matmul(): lax.dot_general(left, right, (((ldim,), (rdim,)), ((), ())), preferred_el...  16.2 us
    all_to_all x1, starting transfers between devices, on_device(): lax.all_to_all(send, DP, 0, 0, tiled=True)  13.2 us
    all_to_all x1, starting transfers between devices, on_device(): everyone = lax.all_to_all(copies, MP, 0, 0, tiled=True)  11.7 us
    all_gather x1, waiting for transfers between devices, on_device(): weights = lax.all_gather(weights, 'z', axis=1, tiled=True)  10.9 us
    ppermute x3, starting transfers between devices, on_device(): gathered.append(lax.ppermute(features, 'x', ring))  9.93 us
  transfers between devices with their start and end apart: 12, of which 9 were waited for; matrix products, arithmetic and copies ran while one was open for 10% of the time, Pallas kernels for 3%

profile of v1, /device:TPU:1, one launch (start us, length us, event | category | flops | bytes accessed | tf_op | source)
XLA Modules:
  0.0 196.7 jit_solution(1967896026260545773)
XLA Ops:
  8.2 17.7 %all-gather = bf16[256,1024]{1,0:T(8,128)(2,1)} all-gather(bf16[64,1024]{1,0:T(8,128)(2,1)S(1)} %pad_maximum_fusion.10), channel_id=2, replica_groups={{0,128,256,384},{64,192,320,448},{1,129,257,385},{65,193,321,449},{2,13..., dimensions={0}, use_global_device_ids=true | all-gather | bytes 655360 | tf_op jit(solution)/shard_map/all_gather | solution.py:156
  27.2 2.1 %fusion = bf16[64,8,1152]{2,1,0:T(8,128)(2,1)} fusion(bf16[128,128]{1,0:T(8,128)(2,1)S(1)} %convolution_convert_fusion.6, bf16[128,512]{1,0:T(8,128)(2,1)S(1)} %get-tuple-element.33, bf16[128,512]{1,0:T(8,128)(2,1)S(1)} %get-tuple-element.32, bf16[128,512]{1,0:T(8,128)(2,1)S(1)} %copy-done.3, bf16[128,512]{1,0:T(8,128)(2,1)S(1)} %copy-done.4, ...), kind=kOutput, calls=%fused_computation.1 | convolution fusion | flops 308871168 | bytes 1756160 | tf_op jit(solution)/shard_map/dot_general | solution.py:17
  29.4 13.2 %all-to-all-start = ((bf16[64,8,1152]{2,1,0:T(8,128)(2,1)}), bf16[64,8,1152]{2,1,0:T(8,128)(2,1)S(1)}, u32[]{:S(2)}, u32[]{:S(2)}) async-start(bf16[64,8,1152]{2,1,0:T(8,128)(2,1)} %fusion), calls=%async_computation | async-start | bytes 2359296 | tf_op jit(solution)/shard_map/all_to_all | solution.py:205
  42.6 25.9 %all-to-all-done = bf16[64,8,1152]{2,1,0:T(8,128)(2,1)S(1)} async-done(((bf16[64,8,1152]{2,1,0:T(8,128)(2,1)}), bf16[64,8,1152]{2,1,0:T(8,128)(2,1)S(1)}, u32[]{:S(2)}, u32[]{:S(2)}) %all-to-all-start) | async-done | bytes 1179680 | tf_op jit(solution)/shard_map/all_to_all | solution.py:205
  69.5 1.6 fusion.10
  72.6 11.7 %all-to-all-start.1 = ((bf16[8,32,512]{2,1,0:T(8,128)(2,1)}), bf16[8,32,512]{2,1,0:T(8,128)(2,1)S(1)}, u32[]{:S(2)}, u32[]{:S(2)}) async-start(bf16[8,32,512]{2,1,0:T(8,128)(2,1)} %broadcast_in_dim.8), calls=%async_computation.1 | async-start | bytes 524288 | tf_op jit(solution)/shard_map/all_to_all | solution.py:224
  84.3 2.8 %collective-permute-start = (bf16[256,1152]{1,0:T(8,128)(2,1)S(1)}, bf16[256,1152]{1,0:T(8,128)(2,1)S(1)}, u32[]{:S(2)}, u32[]{:S(2)}) collective-permute-start(bf16[256,1152]{1,0:T(8,128)(2,1)S(1)} %maximum_maximum_fusion), channel_id=1, source_target_pairs={{0,64},{64,0},{128,192},{192,128},{256,320},{320,256},{384,448},{4... | collective-permute-start | bytes 1769480 | tf_op jit(solution)/shard_map/ppermute | solution.py:186
  87.2 3.7 %all-to-all-done.1 = bf16[8,32,512]{2,1,0:T(8,128)(2,1)S(1)} async-done(((bf16[8,32,512]{2,1,0:T(8,128)(2,1)}), bf16[8,32,512]{2,1,0:T(8,128)(2,1)S(1)}, u32[]{:S(2)}, u32[]{:S(2)}) %all-to-all-start.1) | async-done | bytes 262176 | tf_op jit(solution)/shard_map/all_to_all | solution.py:224
  91.5 1.7 fusion.2
  98.7 2.1 %convolution_multiply_fusion.3 = f32[256,512]{1,0:T(8,128)} fusion(bf16[512,1152]{1,0:T(8,128)(2,1)S(1)} %bitcast.53, bf16[512,512]{1,0:T(8,128)(2,1)} %copy-done.12), kind=kOutput, calls=%fused_computation.24 | convolution fusion | flops 134348800 | bytes 1310720 | tf_op jit(solution)/shard_map/dot_general | solution.py:17
  102.0 10.9 %all-gather.3.cloned.1.call-done.refs_4_.w_ref = bf16[4,512,1024]{2,1,0:T(8,128)(2,1)} async-done(((bf16[4,64,1024]{2,1,0:T(8,128)(2,1)}), bf16[4,512,1024]{2,1,0:T(8,128)(2,1)}) %all-gather.3.cloned.1.call-update) | async-done | bytes 4194320 | tf_op jit(solution)/shard_map/all_gather | solution.py:157
  113.7 5.3 %backward_base.1 = bf16[4,2,2,128,512]{4,3,2,1,0:T(8,128)(2,1)} custom-call(s32[1]{0:T(128)} %bitcast.24.first_ref, bf16[2,128,1152]{2,1,0:T(8,128)(2,1)} %bitcast.44, bf16[2,128,1152]{2,1,0:T(8,128)(2,1)} %bitcast.47, bf16[4,512,1024]{2,1,0:T(8,128)(2,1)} %all-gather.3.cloned.1.call-done.refs_4_.w_ref), custom_call_target="tpu_custom_call" | custom-call | flops 1073741824 | bytes 6291456 | tf_op jit(solution)/shard_map/backward_base/pallas_call | solution.py:110
  119.0 8.5 %all-to-all-start.2 = ((bf16[64,8,1024]{2,1,0:T(8,128)(2,1)}), bf16[64,8,1024]{2,1,0:T(8,128)(2,1)S(1)}, u32[]{:S(2)}, u32[]{:S(2)}) async-start(bf16[64,8,1024]{2,1,0:T(8,128)(2,1)} %bitcast.23), calls=%async_computation.2 | async-start | bytes 2097152 | tf_op jit(solution)/shard_map/all_to_all | solution.py:259
  129.9 2.5 %collective-permute-done.1 = bf16[512,512]{1,0:T(8,128)(2,1)S(1)} collective-permute-done((bf16[512,512]{1,0:T(8,128)(2,1)S(1)}, bf16[512,512]{1,0:T(8,128)(2,1)S(1)}, u32[]{:S(2)}, u32[]{:S(2)}) %collective-permute-start.1) | collective-permute-done | bytes 524320 | tf_op jit(solution)/shard_map/ppermute | solution.py:195
  132.5 3.2 %collective-permute-start.2 = (bf16[512,512]{1,0:T(8,128)(2,1)S(1)}, bf16[512,512]{1,0:T(8,128)(2,1)S(1)}, u32[]{:S(2)}, u32[]{:S(2)}) collective-permute-start(bf16[512,512]{1,0:T(8,128)(2,1)S(1)} %broadcast_select_fusion), channel_id=1, source_target_pairs={{0,2},{2,4},{4,6},{6,0},{1,3},{3,5},{5,7},{7,1},{8,10},{10,12},{12... | collective-permute-start | bytes 1572872 | tf_op jit(solution)/shard_map/ppermute | solution.py:201
  135.7 3.3 %collective-permute-start.3 = (bf16[512,512]{1,0:T(8,128)(2,1)S(1)}, bf16[512,512]{1,0:T(8,128)(2,1)S(1)}, u32[]{:S(2)}, u32[]{:S(2)}) collective-permute-start(bf16[512,512]{1,0:T(8,128)(2,1)S(1)} %broadcast_select_fusion), channel_id=1, source_target_pairs={{0,6},{2,0},{4,2},{6,4},{1,7},{3,1},{5,3},{7,5},{8,14},{10,8},{12,... | collective-permute-start | bytes 1572872 | tf_op jit(solution)/shard_map/ppermute | solution.py:201
  139.0 3.4 %collective-permute-start.4 = (bf16[512,512]{1,0:T(8,128)(2,1)S(1)}, bf16[512,512]{1,0:T(8,128)(2,1)S(1)}, u32[]{:S(2)}, u32[]{:S(2)}) collective-permute-start(bf16[512,512]{1,0:T(8,128)(2,1)S(1)} %broadcast_select_fusion), channel_id=1, source_target_pairs={{0,4},{2,6},{4,0},{6,2},{1,5},{3,7},{5,1},{7,3},{8,12},{10,14},{12... | collective-permute-start | bytes 1572872 | tf_op jit(solution)/shard_map/ppermute | solution.py:201
  143.2 10.5 %collective-permute-done.2 = bf16[512,512]{1,0:T(8,128)(2,1)S(1)} collective-permute-done((bf16[512,512]{1,0:T(8,128)(2,1)S(1)}, bf16[512,512]{1,0:T(8,128)(2,1)S(1)}, u32[]{:S(2)}, u32[]{:S(2)}) %collective-permute-start.2) | collective-permute-done | bytes 524320 | tf_op jit(solution)/shard_map/ppermute | solution.py:201
  153.6 2.5 %collective-permute-done.3 = bf16[512,512]{1,0:T(8,128)(2,1)S(1)} collective-permute-done((bf16[512,512]{1,0:T(8,128)(2,1)S(1)}, bf16[512,512]{1,0:T(8,128)(2,1)S(1)}, u32[]{:S(2)}, u32[]{:S(2)}) %collective-permute-start.3) | collective-permute-done | bytes 524320 | tf_op jit(solution)/shard_map/ppermute | solution.py:201
  156.1 12.0 %collective-permute-done.4 = bf16[512,512]{1,0:T(8,128)(2,1)S(1)} collective-permute-done((bf16[512,512]{1,0:T(8,128)(2,1)S(1)}, bf16[512,512]{1,0:T(8,128)(2,1)S(1)}, u32[]{:S(2)}, u32[]{:S(2)}) %collective-permute-start.4) | collective-permute-done | bytes 524320 | tf_op jit(solution)/shard_map/ppermute | solution.py:201
  169.1 6.2 %forward_base.1 = (f32[2,128,512]{2,1,0:T(8,128)}, bf16[2,128,512]{2,1,0:T(8,128)(2,1)}) custom-call(s32[4]{0:T(128)} %pad_add_fusion.1.order_ref, bf16[2,2,128,512]{3,2,1,0:T(8,128)(2,1)} %bitcast.45, bf16[2,2,128,512]{3,2,1,0:T(8,128)(2,1)} %bitcast.55, bf16[2,2,128,512]{3,2,1,0:T(8,128)(2,1)} %bitcast.56, bf16[2,2,128,512]{3,2,1,0:T(8,128)(2,1)} %bitcast.57, ...), custom_call_target="tpu_custom_call" | custom-call | flops 1073741824 | bytes 6291456 | tf_op jit(solution)/shard_map/forward_base/pallas_call | solution.py:57
  175.2 2.9 %collective-permute-start.5 = (bf16[256,512]{1,0:T(8,128)(2,1)}, bf16[256,512]{1,0:T(8,128)(2,1)S(1)}, u32[]{:S(2)}, u32[]{:S(2)}) collective-permute-start(bf16[256,512]{1,0:T(8,128)(2,1)} %bitcast.67), channel_id=1, source_target_pairs={{0,64},{64,0},{128,192},{192,128},{256,320},{320,256},{384,448},{4... | collective-permute-start | bytes 786440 | tf_op jit(solution)/shard_map/ppermute | solution.py:266
  178.2 3.4 %collective-permute-start.6 = (bf16[256,512]{1,0:T(8,128)(2,1)}, bf16[256,512]{1,0:T(8,128)(2,1)S(1)}, u32[]{:S(2)}, u32[]{:S(2)}) collective-permute-start(bf16[256,512]{1,0:T(8,128)(2,1)} %bitcast.66), channel_id=1, source_target_pairs={{0,0},{1,64},{64,1},{65,65},{128,128},{129,192},{192,129},{193,193... | collective-permute-start | bytes 786440 | tf_op jit(solution)/shard_map/ppermute | solution.py:258
  184.4 3.7 %collective-permute-done.6 = bf16[256,512]{1,0:T(8,128)(2,1)S(1)} collective-permute-done((bf16[256,512]{1,0:T(8,128)(2,1)}, bf16[256,512]{1,0:T(8,128)(2,1)S(1)}, u32[]{:S(2)}, u32[]{:S(2)}) %collective-permute-start.6) | collective-permute-done | bytes 262176 | tf_op jit(solution)/shard_map/ppermute | solution.py:258
  (161 shorter events, 20.9 us)
Async XLA Ops:
  7.2 18.9 %copy-start.40 = (s32[32]{0:T(128)S(1)}, s32[32]{0:T(128)}, u32[]{:S(2)}) copy-start(s32[32]{0:T(128)} %param.22) | copy-start | bytes 388
  7.2 19.1 %copy-start.39 = (s32[32]{0:T(128)S(1)}, s32[32]{0:T(128)}, u32[]{:S(2)}) copy-start(s32[32]{0:T(128)} %param.23) | copy-start | bytes 388
  7.2 19.9 %copy-start.14 = (bf16[128,512]{1,0:T(8,128)(2,1)S(1)}, bf16[128,512]{1,0:T(8,128)(2,1)}, u32[]{:S(2)}) copy-start(bf16[128,512]{1,0:T(8,128)(2,1)} %param.14) | copy-start | bytes 393220
  7.2 19.9 %copy-start.15 = (bf16[128,512]{1,0:T(8,128)(2,1)S(1)}, bf16[128,512]{1,0:T(8,128)(2,1)}, u32[]{:S(2)}) copy-start(bf16[128,512]{1,0:T(8,128)(2,1)} %param.15) | copy-start | bytes 393220
  7.2 105.7 %all-gather.3.cloned.1.call-start = ((), (), s32[]{:S(2)}) async-start(), calls=%async_computation.4 | async-start | bytes 4718592 | tf_op jit(solution)/shard_map/all_gather | solution.py:157
  8.2 19.0 %copy-start.3 = (bf16[128,512]{1,0:T(8,128)(2,1)S(1)}, bf16[128,512]{1,0:T(8,128)(2,1)}, u32[]{:S(2)}) copy-start(bf16[128,512]{1,0:T(8,128)(2,1)} %param.13) | copy-start | bytes 393220
  8.2 19.0 %copy-start.4 = (bf16[128,512]{1,0:T(8,128)(2,1)S(1)}, bf16[128,512]{1,0:T(8,128)(2,1)}, u32[]{:S(2)}) copy-start(bf16[128,512]{1,0:T(8,128)(2,1)} %param.12) | copy-start | bytes 393220
  26.3 42.2 %copy-start.51 = (pred[512]{0:T(512)(128)(4,1)}, pred[512]{0:T(512)(128)(4,1)S(1)}, u32[]{:S(2)}) copy-start(pred[512]{0:T(512)(128)(4,1)S(1)} %fusion.97) | copy-start | bytes 1540
  26.5 42.1 %copy-start.16 = (s32[512]{0:T(512)}, s32[512]{0:T(512)S(1)}, u32[]{:S(2)}) copy-start(s32[512]{0:T(512)S(1)} %get-tuple-element.37) | copy-start | bytes 6148
  26.5 42.0 %copy-start.18 = (s32[512]{0:T(512)}, s32[512]{0:T(512)S(1)}, u32[]{:S(2)}) copy-start(s32[512]{0:T(512)S(1)} %get-tuple-element.46) | copy-start | bytes 6148
  29.4 39.1 %all-to-all-start = ((bf16[64,8,1152]{2,1,0:T(8,128)(2,1)}), bf16[64,8,1152]{2,1,0:T(8,128)(2,1)S(1)}, u32[]{:S(2)}, u32[]{:S(2)}) async-start(bf16[64,8,1152]{2,1,0:T(8,128)(2,1)} %fusion), calls=%async_computation | async-start | bytes 2359296 | tf_op jit(solution)/shard_map/all_to_all | solution.py:205
  72.6 18.2 %all-to-all-start.1 = ((bf16[8,32,512]{2,1,0:T(8,128)(2,1)}), bf16[8,32,512]{2,1,0:T(8,128)(2,1)S(1)}, u32[]{:S(2)}, u32[]{:S(2)}) async-start(bf16[8,32,512]{2,1,0:T(8,128)(2,1)} %broadcast_in_dim.8), calls=%async_computation.1 | async-start | bytes 524288 | tf_op jit(solution)/shard_map/all_to_all | solution.py:224
  84.3 93.9 %reduce-scatter.2.cloned.1.call-start = ((), (), s32[]{:S(2)}) async-start(), calls=%async_computation.5 | async-start | bytes 2359296 | tf_op jit(solution)/shard_map/reduce_scatter | solution.py:257
  84.3 28.5 %collective-permute-start = (bf16[256,1152]{1,0:T(8,128)(2,1)S(1)}, bf16[256,1152]{1,0:T(8,128)(2,1)S(1)}, u32[]{:S(2)}, u32[]{:S(2)}) collective-permute-start(bf16[256,1152]{1,0:T(8,128)(2,1)S(1)} %maximum_maximum_fusion), channel_id=1, source_target_pairs={{0,64},{64,0},{128,192},{192,128},{256,320},{320,256},{384,448},{4... | collective-permute-start | bytes 1769480 | tf_op jit(solution)/shard_map/ppermute | solution.py:186
  119.0 62.5 %all-to-all-start.2 = ((bf16[64,8,1024]{2,1,0:T(8,128)(2,1)}), bf16[64,8,1024]{2,1,0:T(8,128)(2,1)S(1)}, u32[]{:S(2)}, u32[]{:S(2)}) async-start(bf16[64,8,1024]{2,1,0:T(8,128)(2,1)} %bitcast.23), calls=%async_computation.2 | async-start | bytes 2097152 | tf_op jit(solution)/shard_map/all_to_all | solution.py:259
  128.6 3.8 %collective-permute-start.1 = (bf16[512,512]{1,0:T(8,128)(2,1)S(1)}, bf16[512,512]{1,0:T(8,128)(2,1)S(1)}, u32[]{:S(2)}, u32[]{:S(2)}) collective-permute-start(bf16[512,512]{1,0:T(8,128)(2,1)S(1)} %pad_maximum_fusion.1), channel_id=1, source_target_pairs={{0,1},{65,64},{128,129},{193,192},{256,257},{321,320},{384,385},{4... | collective-permute-start | bytes 1572872 | tf_op jit(solution)/shard_map/ppermute | solution.py:195
  132.5 35.7 %copy-start.1 = (bf16[512,512]{1,0:T(8,128)(2,1)}, bf16[512,512]{1,0:T(8,128)(2,1)S(1)}, u32[]{:S(2)}) copy-start(bf16[512,512]{1,0:T(8,128)(2,1)S(1)} %broadcast_select_fusion) | copy-start | bytes 1572868
  132.5 21.1 %collective-permute-start.2 = (bf16[512,512]{1,0:T(8,128)(2,1)S(1)}, bf16[512,512]{1,0:T(8,128)(2,1)S(1)}, u32[]{:S(2)}, u32[]{:S(2)}) collective-permute-start(bf16[512,512]{1,0:T(8,128)(2,1)S(1)} %broadcast_select_fusion), channel_id=1, source_target_pairs={{0,2},{2,4},{4,6},{6,0},{1,3},{3,5},{5,7},{7,1},{8,10},{10,12},{12... | collective-permute-start | bytes 1572872 | tf_op jit(solution)/shard_map/ppermute | solution.py:201
  135.7 20.5 %collective-permute-start.3 = (bf16[512,512]{1,0:T(8,128)(2,1)S(1)}, bf16[512,512]{1,0:T(8,128)(2,1)S(1)}, u32[]{:S(2)}, u32[]{:S(2)}) collective-permute-start(bf16[512,512]{1,0:T(8,128)(2,1)S(1)} %broadcast_select_fusion), channel_id=1, source_target_pairs={{0,6},{2,0},{4,2},{6,4},{1,7},{3,1},{5,3},{7,5},{8,14},{10,8},{12,... | collective-permute-start | bytes 1572872 | tf_op jit(solution)/shard_map/ppermute | solution.py:201
  139.0 29.1 %collective-permute-start.4 = (bf16[512,512]{1,0:T(8,128)(2,1)S(1)}, bf16[512,512]{1,0:T(8,128)(2,1)S(1)}, u32[]{:S(2)}, u32[]{:S(2)}) collective-permute-start(bf16[512,512]{1,0:T(8,128)(2,1)S(1)} %broadcast_select_fusion), channel_id=1, source_target_pairs={{0,4},{2,6},{4,0},{6,2},{1,5},{3,7},{5,1},{7,3},{8,12},{10,14},{12... | collective-permute-start | bytes 1572872 | tf_op jit(solution)/shard_map/ppermute | solution.py:201
  153.6 14.5 %copy-start.6 = (bf16[512,512]{1,0:T(8,128)(2,1)}, bf16[512,512]{1,0:T(8,128)(2,1)S(1)}, u32[]{:S(2)}) copy-start(bf16[512,512]{1,0:T(8,128)(2,1)S(1)} %collective-permute-done.2) | copy-start | bytes 1572868
  168.9 12.7 %copy-start.25 = (s32[512]{0:T(512)S(1)}, s32[512]{0:T(512)}, u32[]{:S(2)}) copy-start(s32[512]{0:T(512)} %copy-done.24) | copy-start | bytes 6148
  175.2 9.2 %collective-permute-start.5 = (bf16[256,512]{1,0:T(8,128)(2,1)}, bf16[256,512]{1,0:T(8,128)(2,1)S(1)}, u32[]{:S(2)}, u32[]{:S(2)}) collective-permute-start(bf16[256,512]{1,0:T(8,128)(2,1)} %bitcast.67), channel_id=1, source_target_pairs={{0,64},{64,0},{128,192},{192,128},{256,320},{320,256},{384,448},{4... | collective-permute-start | bytes 786440 | tf_op jit(solution)/shard_map/ppermute | solution.py:266
  178.2 10.0 %collective-permute-start.6 = (bf16[256,512]{1,0:T(8,128)(2,1)}, bf16[256,512]{1,0:T(8,128)(2,1)S(1)}, u32[]{:S(2)}, u32[]{:S(2)}) collective-permute-start(bf16[256,512]{1,0:T(8,128)(2,1)} %bitcast.66), channel_id=1, source_target_pairs={{0,0},{1,64},{64,1},{65,65},{128,128},{129,192},{192,129},{193,193... | collective-permute-start | bytes 786440 | tf_op jit(solution)/shard_map/ppermute | solution.py:258
  (41 other events, 275.3 us)
Sparse Core Ops, SparseCore 0:
  26.1 86.7 all-gather.2
  119.1 38.7 reduce-scatter.1

commit v2 on v1

--- a/solution.py
+++ b/solution.py
@@ -78,7 +78,7 @@
     )(order, *rows, weights)
 
 
-def backward_kernel(first_ref, own_ref, other_ref, w_ref, out_ref, part):
+def backward_kernel(first_ref, own_ref, other_ref, w_ref, kept_ref, sent_ref, part):
     sides, tokens, width = own_ref.shape
     for w in range(sides):
         rows = jnp.concatenate([own_ref[w], other_ref[w]], axis=0)
@@ -92,13 +92,13 @@
 
     @pl.when(own_first)
     def _():
-        out_ref[0, 0] = part[:, :tokens].astype(BF16)
-        out_ref[0, 1] = part[:, tokens:].astype(BF16)
+        kept_ref[0] = part[:, :tokens].astype(BF16)
+        sent_ref[0] = part[:, tokens:].astype(BF16)
 
     @pl.when(jnp.logical_not(own_first))
     def _():
-        out_ref[0, 0] = part[:, tokens:].astype(BF16)
-        out_ref[0, 1] = part[:, :tokens].astype(BF16)
+        kept_ref[0] = part[:, tokens:].astype(BF16)
+        sent_ref[0] = part[:, :tokens].astype(BF16)
 
 
 def backward_base(first, own, other, weights):
@@ -106,17 +106,17 @@
     sides, tokens, _ = own.shape
     width = wide // sides
     rows = pl.BlockSpec((sides, tokens, width), lambda k, first: (0, 0, 1))
-    out = pl.BlockSpec((1, 2, sides, tokens, depth), lambda k, first: (k, 0, 0, 0, 0))
+    out = pl.BlockSpec((1, sides, tokens, depth), lambda k, first: (k, 0, 0, 0))
     return pl.pallas_call(
         backward_kernel,
         grid_spec=pltpu.PrefetchScalarGridSpec(
             num_scalar_prefetch=1,
             grid=(steps,),
             in_specs=[rows, rows, pl.BlockSpec((1, depth, wide), lambda k, first: (k, 0, 0))],
-            out_specs=out,
+            out_specs=[out, out],
             scratch_shapes=[pltpu.VMEM((sides, 2 * tokens, depth), F32)],
         ),
-        out_shape=jax.ShapeDtypeStruct((steps, 2, sides, tokens, depth), BF16),
+        out_shape=[jax.ShapeDtypeStruct((steps, sides, tokens, depth), BF16)] * 2,
         compiler_params=pltpu.CompilerParams(dimension_semantics=("arbitrary",)),
         cost_estimate=pl.CostEstimate(
             flops=4 * tokens * steps * depth * wide,
@@ -243,23 +243,26 @@
 
     gradients = (narrower_gradient, widener_gradient, reducer_gradient, enlarger_gradient)
     raised = raised.reshape(owners, 2 * rows, 2 * width)
-    gradients, weights = lax.optimization_barrier((gradients, weights))
-
-    wide = payload.shape[1]
-    chunks = backward_base(
-        odd.astype(jnp.int32).reshape(1),
-        payload.reshape(2, tokens, wide),
-        other.reshape(2, tokens, wide),
-        weights,
-    )
-    chunks = chunks.reshape(nx * nc, both, width)
-    raised, chunks = lax.optimization_barrier((raised, chunks))
-    total = lax.psum_scatter(chunks, MP, scatter_dimension=0, tiled=False)
-    total = lax.ppermute(total, ("y", "c"), trade).astype(F32)
+    gradients, raised = lax.optimization_barrier((gradients, raised))
     back = lax.all_to_all(
         raised, DP, 0, 0, tiled=True
     ).reshape(slot_rows, 2 * width)
     terms = matmul(table, back, 0, 0)
+
+    wide = payload.shape[1]
+    kept, sent = backward_base(
+        (c ^ odd).astype(jnp.int32).reshape(1),
+        payload.reshape(2, tokens, wide),
+        other.reshape(2, tokens, wide),
+        weights,
+    )
+    kept = kept.reshape(nx, both, width)
+    sent = sent.reshape(nx, both, width)
+    got = lax.ppermute(sent, "c", [(0, 1), (1, 0)])
+
+    pair = (kept.astype(F32) + got.astype(F32)).astype(BF16)
+    total = lax.psum_scatter(pair, "x", scatter_dimension=0, tiled=False)
+    total = lax.ppermute(total, ("y", "c"), trade).astype(F32)
 
     keep, give = forward_base(order, features, weights)
     keep = keep.reshape(both, width)

time: 198 us -> 205 us (1.035)
  starting transfers between devices: 53.7 us -> 56.1 us
    ppermute x1, waiting for transfers between devices: 0.01 us -> 5.83 us  [on_device(): other = lax.ppermute(payload, 'y', neighbour)]
    ppermute x3, waiting for transfers between devices: 25 us -> 19.5 us  [on_device(): gathered.append(lax.ppermute(features, 'x', ring))]
    ppermute x0 -> x1, starting transfers between devices: none -> 2.49 us  [on_device(): got = lax.ppermute(sent, 'c', [(0, 1), (1, 0)])]
  transfers between devices with their start and end apart: 12 -> 13, of which waited for: 9 -> 8; matrix products, arithmetic and copies ran while one was open for 10% -> 11% of each run, Pallas kernels for 3% -> 3%
where the time goes in v2:
time: 205 us; the launch traced here: 204 us
  waiting for transfers between devices  74.6 us (36%)
  starting transfers between devices  56.1 us (27%)
  matrix products  17.8 us (9%)
  blocking collectives  17.7 us (9%)
  between operations  14.5 us (7%)
  Pallas kernels  11.5 us (6%)
  local copies, waits for them, and re-layouts  7.6 us (4%)
  other arithmetic  3.71 us (2%)
    all_to_all x1, waiting for transfers between devices, on_device(): lax.all_to_all(send, DP, 0, 0, tiled=True)  25.8 us
    ppermute x3, waiting for transfers between devices, on_device(): gathered.append(lax.ppermute(features, 'x', ring))  19.5 us
    dot_general x16, matrix products, matmul(): lax.dot_general(left, right, (((ldim,), (rdim,)), ((), ())), preferred_el...  17.8 us
    all_gather x1, blocking collectives, on_device(): lax.all_gather(weights, 'y', axis=0, axis_index_groups=same_parity)  17.7 us
    all_to_all x1, starting transfers between devices, on_device(): lax.all_to_all(send, DP, 0, 0, tiled=True)  13.2 us
    all_to_all x1, starting transfers between devices, on_device(): everyone = lax.all_to_all(copies, MP, 0, 0, tiled=True)  11.8 us
    all_gather x1, waiting for transfers between devices, on_device(): weights = lax.all_gather(weights, 'z', axis=1, tiled=True)  11.7 us
    ppermute x3, starting transfers between devices, on_device(): gathered.append(lax.ppermute(features, 'x', ring))  9.92 us
  transfers between devices with their start and end apart: 13, of which 8 were waited for; matrix products, arithmetic and copies ran while one was open for 11% of the time, Pallas kernels for 3%

profile of v2, /device:TPU:1, one launch (start us, length us, event | category | flops | bytes accessed | tf_op | source)
XLA Modules:
  0.0 203.6 jit_solution(15620707177417950916)
XLA Ops:
  8.2 17.7 %all-gather = bf16[256,1024]{1,0:T(8,128)(2,1)} all-gather(bf16[64,1024]{1,0:T(8,128)(2,1)S(1)} %pad_maximum_fusion.10), channel_id=2, replica_groups={{0,128,256,384},{64,192,320,448},{1,129,257,385},{65,193,321,449},{2,13..., dimensions={0}, use_global_device_ids=true | all-gather | bytes 655360 | tf_op jit(solution)/shard_map/all_gather | solution.py:156
  27.0 2.1 %fusion = bf16[64,8,1152]{2,1,0:T(8,128)(2,1)} fusion(bf16[128,128]{1,0:T(8,128)(2,1)S(1)} %convolution_convert_fusion.6, bf16[128,512]{1,0:T(8,128)(2,1)S(1)} %get-tuple-element.33, bf16[128,512]{1,0:T(8,128)(2,1)S(1)} %get-tuple-element.32, bf16[128,512]{1,0:T(8,128)(2,1)S(1)} %copy-done.3, bf16[128,512]{1,0:T(8,128)(2,1)S(1)} %copy-done.4, ...), kind=kOutput, calls=%fused_computation.1 | convolution fusion | flops 308871168 | bytes 1756160 | tf_op jit(solution)/shard_map/dot_general | solution.py:17
  29.2 13.2 %all-to-all-start = ((bf16[64,8,1152]{2,1,0:T(8,128)(2,1)}), bf16[64,8,1152]{2,1,0:T(8,128)(2,1)S(1)}, u32[]{:S(2)}, u32[]{:S(2)}) async-start(bf16[64,8,1152]{2,1,0:T(8,128)(2,1)} %fusion), calls=%async_computation | async-start | bytes 2359296 | tf_op jit(solution)/shard_map/all_to_all | solution.py:205
  42.4 25.8 %all-to-all-done = bf16[64,8,1152]{2,1,0:T(8,128)(2,1)S(1)} async-done(((bf16[64,8,1152]{2,1,0:T(8,128)(2,1)}), bf16[64,8,1152]{2,1,0:T(8,128)(2,1)S(1)}, u32[]{:S(2)}, u32[]{:S(2)}) %all-to-all-start) | async-done | bytes 1179680 | tf_op jit(solution)/shard_map/all_to_all | solution.py:205
  72.3 11.8 %all-to-all-start.1 = ((bf16[8,32,512]{2,1,0:T(8,128)(2,1)}), bf16[8,32,512]{2,1,0:T(8,128)(2,1)S(1)}, u32[]{:S(2)}, u32[]{:S(2)}) async-start(bf16[8,32,512]{2,1,0:T(8,128)(2,1)} %broadcast_in_dim.8), calls=%async_computation.1 | async-start | bytes 524288 | tf_op jit(solution)/shard_map/all_to_all | solution.py:224
  84.1 2.8 %collective-permute-start = (bf16[256,1152]{1,0:T(8,128)(2,1)S(1)}, bf16[256,1152]{1,0:T(8,128)(2,1)S(1)}, u32[]{:S(2)}, u32[]{:S(2)}) collective-permute-start(bf16[256,1152]{1,0:T(8,128)(2,1)S(1)} %maximum_maximum_fusion), channel_id=1, source_target_pairs={{0,64},{64,0},{128,192},{192,128},{256,320},{320,256},{384,448},{4... | collective-permute-start | bytes 1769480 | tf_op jit(solution)/shard_map/ppermute | solution.py:186
  86.9 3.7 %all-to-all-done.1 = bf16[8,32,512]{2,1,0:T(8,128)(2,1)S(1)} async-done(((bf16[8,32,512]{2,1,0:T(8,128)(2,1)}), bf16[8,32,512]{2,1,0:T(8,128)(2,1)S(1)}, u32[]{:S(2)}, u32[]{:S(2)}) %all-to-all-start.1) | async-done | bytes 262176 | tf_op jit(solution)/shard_map/all_to_all | solution.py:224
  91.2 2.6 %fusion.2 = bf16[512,512]{0,1:T(8,128)(2,1)} fusion(bf16[512,512]{1,0:T(8,128)(2,1)S(1)} %fusion.6, bf16[256,512]{1,0:T(8,128)(2,1)} %bitcast.61, bf16[256,512]{1,0:T(8,128)(2,1)} %bitcast.63), kind=kOutput, calls=%fused_computation.13 | convolution fusion | flops 270008320 | bytes 1572864 | tf_op jit(solution)/shard_map/dot_general | solution.py:17
  95.1 5.8 %collective-permute-done = bf16[256,1152]{1,0:T(8,128)(2,1)S(1)} collective-permute-done((bf16[256,1152]{1,0:T(8,128)(2,1)S(1)}, bf16[256,1152]{1,0:T(8,128)(2,1)S(1)}, u32[]{:S(2)}, u32[]{:S(2)}) %collective-permute-start) | collective-permute-done | bytes 589856 | tf_op jit(solution)/shard_map/ppermute | solution.py:186
  100.9 11.7 %all-gather.3.cloned.1.call-done.refs_4_.w_ref = bf16[4,512,1024]{2,1,0:T(8,128)(2,1)} async-done(((bf16[4,64,1024]{2,1,0:T(8,128)(2,1)}), bf16[4,512,1024]{2,1,0:T(8,128)(2,1)}) %all-gather.3.cloned.1.call-update) | async-done | bytes 4194320 | tf_op jit(solution)/shard_map/all_gather | solution.py:157
  112.7 5.4 %backward_base.1 = (bf16[4,2,128,512]{3,2,1,0:T(8,128)(2,1)}, bf16[4,2,128,512]{3,2,1,0:T(8,128)(2,1)}) custom-call(s32[1]{0:T(128)} %bitcast.25.first_ref, bf16[2,128,1152]{2,1,0:T(8,128)(2,1)} %bitcast.46, bf16[2,128,1152]{2,1,0:T(8,128)(2,1)} %bitcast.49, bf16[4,512,1024]{2,1,0:T(8,128)(2,1)} %all-gather.3.cloned.1.call-done.refs_4_.w_ref), custom_call_target="tpu_custom_call" | custom-call | flops 1073741824 | bytes 6291456 | tf_op jit(solution)/shard_map/backward_base/pallas_call | solution.py:110
  118.0 2.5 %collective-permute-start.6 = (bf16[4,256,512]{2,1,0:T(8,128)(2,1)}, bf16[4,256,512]{2,1,0:T(8,128)(2,1)S(1)}, u32[]{:S(2)}, u32[]{:S(2)}) collective-permute-start(bf16[4,256,512]{2,1,0:T(8,128)(2,1)} %bitcast.60), channel_id=1, source_target_pairs={{0,1},{1,0},{2,3},{3,2},{4,5},{5,4},{6,7},{7,6},{8,9},{9,8},{10,11... | collective-permute-start | bytes 3145736 | tf_op jit(solution)/shard_map/ppermute | solution.py:261
  120.6 2.2 %fusion.3 = bf16[512,512]{0,1:T(8,128)(2,1)} fusion(bf16[512,512]{1,0:T(8,128)(2,1)S(1)} %copy-done.10, bf16[256,512]{1,0:T(8,128)(2,1)S(1)} %bitcast.66, bf16[256,512]{1,0:T(8,128)(2,1)} %bitcast.68), kind=kOutput, calls=%fused_computation.14 | convolution fusion | flops 270008320 | bytes 1572864 | tf_op jit(solution)/shard_map/dot_general | solution.py:17
  131.2 8.5 %all-to-all-start.2 = ((bf16[64,8,1024]{2,1,0:T(8,128)(2,1)}), bf16[64,8,1024]{2,1,0:T(8,128)(2,1)S(1)}, u32[]{:S(2)}, u32[]{:S(2)}) async-start(bf16[64,8,1024]{2,1,0:T(8,128)(2,1)} %bitcast.23), calls=%async_computation.2 | async-start | bytes 2097152 | tf_op jit(solution)/shard_map/all_to_all | solution.py:247
  142.0 2.5 %collective-permute-done.1 = bf16[512,512]{1,0:T(8,128)(2,1)S(1)} collective-permute-done((bf16[512,512]{1,0:T(8,128)(2,1)S(1)}, bf16[512,512]{1,0:T(8,128)(2,1)S(1)}, u32[]{:S(2)}, u32[]{:S(2)}) %collective-permute-start.1) | collective-permute-done | bytes 524320 | tf_op jit(solution)/shard_map/ppermute | solution.py:195
  144.7 3.1 %collective-permute-start.2 = (bf16[512,512]{1,0:T(8,128)(2,1)S(1)}, bf16[512,512]{1,0:T(8,128)(2,1)S(1)}, u32[]{:S(2)}, u32[]{:S(2)}) collective-permute-start(bf16[512,512]{1,0:T(8,128)(2,1)S(1)} %broadcast_select_fusion), channel_id=1, source_target_pairs={{0,2},{2,4},{4,6},{6,0},{1,3},{3,5},{5,7},{7,1},{8,10},{10,12},{12... | collective-permute-start | bytes 1572872 | tf_op jit(solution)/shard_map/ppermute | solution.py:201
  147.8 3.4 %collective-permute-start.3 = (bf16[512,512]{1,0:T(8,128)(2,1)S(1)}, bf16[512,512]{1,0:T(8,128)(2,1)S(1)}, u32[]{:S(2)}, u32[]{:S(2)}) collective-permute-start(bf16[512,512]{1,0:T(8,128)(2,1)S(1)} %broadcast_select_fusion), channel_id=1, source_target_pairs={{0,6},{2,0},{4,2},{6,4},{1,7},{3,1},{5,3},{7,5},{8,14},{10,8},{12,... | collective-permute-start | bytes 1572872 | tf_op jit(solution)/shard_map/ppermute | solution.py:201
  151.2 3.4 %collective-permute-start.4 = (bf16[512,512]{1,0:T(8,128)(2,1)S(1)}, bf16[512,512]{1,0:T(8,128)(2,1)S(1)}, u32[]{:S(2)}, u32[]{:S(2)}) collective-permute-start(bf16[512,512]{1,0:T(8,128)(2,1)S(1)} %broadcast_select_fusion), channel_id=1, source_target_pairs={{0,4},{2,6},{4,0},{6,2},{1,5},{3,7},{5,1},{7,3},{8,12},{10,14},{12... | collective-permute-start | bytes 1572872 | tf_op jit(solution)/shard_map/ppermute | solution.py:201
  155.3 19.5 %collective-permute-done.2 = bf16[512,512]{1,0:T(8,128)(2,1)S(1)} collective-permute-done((bf16[512,512]{1,0:T(8,128)(2,1)S(1)}, bf16[512,512]{1,0:T(8,128)(2,1)S(1)}, u32[]{:S(2)}, u32[]{:S(2)}) %collective-permute-start.2) | collective-permute-done | bytes 524320 | tf_op jit(solution)/shard_map/ppermute | solution.py:201
  176.1 6.1 %forward_base.1 = (f32[2,128,512]{2,1,0:T(8,128)}, bf16[2,128,512]{2,1,0:T(8,128)(2,1)}) custom-call(s32[4]{0:T(128)} %pad_add_fusion.1.order_ref, bf16[2,2,128,512]{3,2,1,0:T(8,128)(2,1)} %bitcast.47, bf16[2,2,128,512]{3,2,1,0:T(8,128)(2,1)} %bitcast.57, bf16[2,2,128,512]{3,2,1,0:T(8,128)(2,1)} %bitcast.58, bf16[2,2,128,512]{3,2,1,0:T(8,128)(2,1)} %bitcast.59, ...), custom_call_target="tpu_custom_call" | custom-call | flops 1073741824 | bytes 6291456 | tf_op jit(solution)/shard_map/forward_base/pallas_call | solution.py:57
  182.2 3.0 %collective-permute-start.5 = (bf16[256,512]{1,0:T(8,128)(2,1)}, bf16[256,512]{1,0:T(8,128)(2,1)S(1)}, u32[]{:S(2)}, u32[]{:S(2)}) collective-permute-start(bf16[256,512]{1,0:T(8,128)(2,1)} %bitcast.70), channel_id=1, source_target_pairs={{0,64},{64,0},{128,192},{192,128},{256,320},{320,256},{384,448},{4... | collective-permute-start | bytes 786440 | tf_op jit(solution)/shard_map/ppermute | solution.py:269
  185.3 3.1 %collective-permute-start.7 = (bf16[256,512]{1,0:T(8,128)(2,1)}, bf16[256,512]{1,0:T(8,128)(2,1)S(1)}, u32[]{:S(2)}, u32[]{:S(2)}) collective-permute-start(bf16[256,512]{1,0:T(8,128)(2,1)} %bitcast.69), channel_id=1, source_target_pairs={{0,0},{1,64},{64,1},{65,65},{128,128},{129,192},{192,129},{193,193... | collective-permute-start | bytes 786440 | tf_op jit(solution)/shard_map/ppermute | solution.py:265
  189.6 2.0 collective-permute-done.5
  191.5 3.6 %collective-permute-done.7 = bf16[256,512]{1,0:T(8,128)(2,1)S(1)} collective-permute-done((bf16[256,512]{1,0:T(8,128)(2,1)}, bf16[256,512]{1,0:T(8,128)(2,1)S(1)}, u32[]{:S(2)}, u32[]{:S(2)}) %collective-permute-start.7) | collective-permute-done | bytes 262176 | tf_op jit(solution)/shard_map/ppermute | solution.py:265
  (104 shorter events, 23.6 us)
Async XLA Ops:
  7.2 18.8 %copy-start.21 = (s32[32]{0:T(128)S(1)}, s32[32]{0:T(128)}, u32[]{:S(2)}) copy-start(s32[32]{0:T(128)} %param.23) | copy-start | bytes 388
  7.2 18.9 %copy-start.22 = (s32[32]{0:T(128)S(1)}, s32[32]{0:T(128)}, u32[]{:S(2)}) copy-start(s32[32]{0:T(128)} %param.22) | copy-start | bytes 388
  7.2 19.7 %copy-start.15 = (bf16[128,512]{1,0:T(8,128)(2,1)S(1)}, bf16[128,512]{1,0:T(8,128)(2,1)}, u32[]{:S(2)}) copy-start(bf16[128,512]{1,0:T(8,128)(2,1)} %param.14) | copy-start | bytes 393220
  7.2 19.7 %copy-start.16 = (bf16[128,512]{1,0:T(8,128)(2,1)S(1)}, bf16[128,512]{1,0:T(8,128)(2,1)}, u32[]{:S(2)}) copy-start(bf16[128,512]{1,0:T(8,128)(2,1)} %param.15) | copy-start | bytes 393220
  7.2 105.4 %all-gather.3.cloned.1.call-start = ((), (), s32[]{:S(2)}) async-start(), calls=%async_computation.4 | async-start | bytes 4718592 | tf_op jit(solution)/shard_map/all_gather | solution.py:157
  8.2 18.8 %copy-start.3 = (bf16[128,512]{1,0:T(8,128)(2,1)S(1)}, bf16[128,512]{1,0:T(8,128)(2,1)}, u32[]{:S(2)}) copy-start(bf16[128,512]{1,0:T(8,128)(2,1)} %param.13) | copy-start | bytes 393220
  8.2 18.8 %copy-start.4 = (bf16[128,512]{1,0:T(8,128)(2,1)S(1)}, bf16[128,512]{1,0:T(8,128)(2,1)}, u32[]{:S(2)}) copy-start(bf16[128,512]{1,0:T(8,128)(2,1)} %param.12) | copy-start | bytes 393220
  29.2 39.0 %all-to-all-start = ((bf16[64,8,1152]{2,1,0:T(8,128)(2,1)}), bf16[64,8,1152]{2,1,0:T(8,128)(2,1)S(1)}, u32[]{:S(2)}, u32[]{:S(2)}) async-start(bf16[64,8,1152]{2,1,0:T(8,128)(2,1)} %fusion), calls=%async_computation | async-start | bytes 2359296 | tf_op jit(solution)/shard_map/all_to_all | solution.py:205
  72.3 18.3 %all-to-all-start.1 = ((bf16[8,32,512]{2,1,0:T(8,128)(2,1)}), bf16[8,32,512]{2,1,0:T(8,128)(2,1)S(1)}, u32[]{:S(2)}, u32[]{:S(2)}) async-start(bf16[8,32,512]{2,1,0:T(8,128)(2,1)} %broadcast_in_dim.8), calls=%async_computation.1 | async-start | bytes 524288 | tf_op jit(solution)/shard_map/all_to_all | solution.py:224
  84.0 101.2 %reduce-scatter.2.cloned.1.call-start = ((), (), s32[]{:S(2)}) async-start(), calls=%async_computation.5 | async-start | bytes 1310720 | tf_op jit(solution)/shard_map/reduce_scatter | solution.py:264
  84.1 9.7 %copy-start = (bf16[256,1152]{1,0:T(8,128)(2,1)}, bf16[256,1152]{1,0:T(8,128)(2,1)S(1)}, u32[]{:S(2)}) copy-start(bf16[256,1152]{1,0:T(8,128)(2,1)S(1)} %maximum_maximum_fusion) | copy-start | bytes 1769476
  84.1 16.8 %collective-permute-start = (bf16[256,1152]{1,0:T(8,128)(2,1)S(1)}, bf16[256,1152]{1,0:T(8,128)(2,1)S(1)}, u32[]{:S(2)}, u32[]{:S(2)}) collective-permute-start(bf16[256,1152]{1,0:T(8,128)(2,1)S(1)} %maximum_maximum_fusion), channel_id=1, source_target_pairs={{0,64},{64,0},{128,192},{192,128},{256,320},{320,256},{384,448},{4... | collective-permute-start | bytes 1769480 | tf_op jit(solution)/shard_map/ppermute | solution.py:186
  100.9 11.7 %copy-start.2 = (bf16[256,1152]{1,0:T(8,128)(2,1)}, bf16[256,1152]{1,0:T(8,128)(2,1)S(1)}, u32[]{:S(2)}) copy-start(bf16[256,1152]{1,0:T(8,128)(2,1)S(1)} %collective-permute-done) | copy-start | bytes 1769476
  112.7 7.9 %copy-start.20 = (bf16[16,16,512]{2,1,0:T(8,128)(2,1)S(1)}, bf16[16,16,512]{2,1,0:T(8,128)(2,1)}, u32[]{:S(2)}) copy-start(bf16[16,16,512]{2,1,0:T(8,128)(2,1)} %param.20) | copy-start | bytes 786436
  118.0 9.2 %collective-permute-start.6 = (bf16[4,256,512]{2,1,0:T(8,128)(2,1)}, bf16[4,256,512]{2,1,0:T(8,128)(2,1)S(1)}, u32[]{:S(2)}, u32[]{:S(2)}) collective-permute-start(bf16[4,256,512]{2,1,0:T(8,128)(2,1)} %bitcast.60), channel_id=1, source_target_pairs={{0,1},{1,0},{2,3},{3,2},{4,5},{5,4},{6,7},{7,6},{8,9},{9,8},{10,11... | collective-permute-start | bytes 3145736 | tf_op jit(solution)/shard_map/ppermute | solution.py:261
  131.2 57.2 %all-to-all-start.2 = ((bf16[64,8,1024]{2,1,0:T(8,128)(2,1)}), bf16[64,8,1024]{2,1,0:T(8,128)(2,1)S(1)}, u32[]{:S(2)}, u32[]{:S(2)}) async-start(bf16[64,8,1024]{2,1,0:T(8,128)(2,1)} %bitcast.23), calls=%async_computation.2 | async-start | bytes 2097152 | tf_op jit(solution)/shard_map/all_to_all | solution.py:247
  140.7 3.8 %collective-permute-start.1 = (bf16[512,512]{1,0:T(8,128)(2,1)S(1)}, bf16[512,512]{1,0:T(8,128)(2,1)S(1)}, u32[]{:S(2)}, u32[]{:S(2)}) collective-permute-start(bf16[512,512]{1,0:T(8,128)(2,1)S(1)} %pad_maximum_fusion.1), channel_id=1, source_target_pairs={{0,1},{65,64},{128,129},{193,192},{256,257},{321,320},{384,385},{4... | collective-permute-start | bytes 1572872 | tf_op jit(solution)/shard_map/ppermute | solution.py:195
  144.7 30.2 %copy-start.1 = (bf16[512,512]{1,0:T(8,128)(2,1)}, bf16[512,512]{1,0:T(8,128)(2,1)S(1)}, u32[]{:S(2)}) copy-start(bf16[512,512]{1,0:T(8,128)(2,1)S(1)} %broadcast_select_fusion) | copy-start | bytes 1572868
  144.7 30.1 %collective-permute-start.2 = (bf16[512,512]{1,0:T(8,128)(2,1)S(1)}, bf16[512,512]{1,0:T(8,128)(2,1)S(1)}, u32[]{:S(2)}, u32[]{:S(2)}) collective-permute-start(bf16[512,512]{1,0:T(8,128)(2,1)S(1)} %broadcast_select_fusion), channel_id=1, source_target_pairs={{0,2},{2,4},{4,6},{6,0},{1,3},{3,5},{5,7},{7,1},{8,10},{10,12},{12... | collective-permute-start | bytes 1572872 | tf_op jit(solution)/shard_map/ppermute | solution.py:201
  147.8 27.0 %collective-permute-start.3 = (bf16[512,512]{1,0:T(8,128)(2,1)S(1)}, bf16[512,512]{1,0:T(8,128)(2,1)S(1)}, u32[]{:S(2)}, u32[]{:S(2)}) collective-permute-start(bf16[512,512]{1,0:T(8,128)(2,1)S(1)} %broadcast_select_fusion), channel_id=1, source_target_pairs={{0,6},{2,0},{4,2},{6,4},{1,7},{3,1},{5,3},{7,5},{8,14},{10,8},{12,... | collective-permute-start | bytes 1572872 | tf_op jit(solution)/shard_map/ppermute | solution.py:201
  151.2 23.6 %collective-permute-start.4 = (bf16[512,512]{1,0:T(8,128)(2,1)S(1)}, bf16[512,512]{1,0:T(8,128)(2,1)S(1)}, u32[]{:S(2)}, u32[]{:S(2)}) collective-permute-start(bf16[512,512]{1,0:T(8,128)(2,1)S(1)} %broadcast_select_fusion), channel_id=1, source_target_pairs={{0,4},{2,6},{4,0},{6,2},{1,5},{3,7},{5,1},{7,3},{8,12},{10,14},{12... | collective-permute-start | bytes 1572872 | tf_op jit(solution)/shard_map/ppermute | solution.py:201
  182.2 9.3 %collective-permute-start.5 = (bf16[256,512]{1,0:T(8,128)(2,1)}, bf16[256,512]{1,0:T(8,128)(2,1)S(1)}, u32[]{:S(2)}, u32[]{:S(2)}) collective-permute-start(bf16[256,512]{1,0:T(8,128)(2,1)} %bitcast.70), channel_id=1, source_target_pairs={{0,64},{64,0},{128,192},{192,128},{256,320},{320,256},{384,448},{4... | collective-permute-start | bytes 786440 | tf_op jit(solution)/shard_map/ppermute | solution.py:269
  185.3 9.9 %copy-start.9 = (f32[2,128,512]{2,1,0:T(8,128)S(1)}, f32[2,128,512]{2,1,0:T(8,128)}, u32[]{:S(2)}) copy-start(f32[2,128,512]{2,1,0:T(8,128)} %get-tuple-element.17) | copy-start | bytes 1572868
  185.3 9.8 %collective-permute-start.7 = (bf16[256,512]{1,0:T(8,128)(2,1)}, bf16[256,512]{1,0:T(8,128)(2,1)S(1)}, u32[]{:S(2)}, u32[]{:S(2)}) collective-permute-start(bf16[256,512]{1,0:T(8,128)(2,1)} %bitcast.69), channel_id=1, source_target_pairs={{0,0},{1,64},{64,1},{65,65},{128,128},{129,192},{192,129},{193,193... | collective-permute-start | bytes 786440 | tf_op jit(solution)/shard_map/ppermute | solution.py:265
  (12 other events, 28.4 us)
Sparse Core Ops, SparseCore 0:
  26.1 86.5 all-gather.2
  128.8 25.0 reduce-scatter.1
